TPU v7x, 512 devices: a whole 4x4x16 slice. The times are simulated.
512 devices in a mesh: beam: 16 (over z), pulse: 4 (over x), range: 8 (over y, core).
Axes of the slice: x: 4, y: 4, z: 16, core: 2. Of those that a mesh axis runs over, the one named last changes fastest.
Arguments:
- signal: bfloat16 [32, 32, 2, 4096], P('beam', 'pulse', None, 'range'), may hold values from -40 to 40, as said below
- replica: bfloat16 [2, 2048], P(None, ('beam', 'pulse')), may hold values from -0.09375 to 0.09375
- guard_cells: int32 [32], P('beam'), may hold values from 1 to 8, as said below
- train_cells: int32 [32], P('beam'), may hold values from 64 to 96, as said below
- scale_index: int32 [32], P('beam'), may hold values from 0 to 15
- offsets: int32 [32], P('beam'), may hold values from 0 to 127, as said below
Outputs:
- compressed: bfloat16 [32, 32, 2, 4096], P('beam', 'pulse', None, 'range')
- test_ratio: float32 [32, 32, 4096], P('beam', 'pulse', 'range')
Inputs may be any that keep to these rules, and one draw needn't show every extreme that they name: `signal`: values stay within the range, with cell-to-cell varying levels. `guard_cells`: some beam has exactly 8 guard cells. `train_cells`: the beam with 8 guard cells has 96 training cells. `offsets`: some beam has the offset 128 - 1.
All inputs are finite; a program needn't handle non-finite values.
Results may differ from a plain program's by a relative error of at most 0.001.
Values may be sent and summed in bfloat16 or wider, within the bound.
No kernel may reach another device: no remote copies, remote signals or barrier semaphores. Data moves between devices by JAX's collectives and lax.ppermute only.
A program may use at most 64 MiB of HBM per device.

v0:
```python
import jax
import jax.numpy as jnp
from jax import lax
from jax.sharding import PartitionSpec as P

TILE = 128
OFF_MAX = 128
GUARD_MAX = 8
TRAIN_MAX = 96


EPSILON = 1e-06


def joined_along(tiles, dim):
    tiles = jnp.moveaxis(tiles, 0, dim)
    lengths = tiles.shape
    return tiles.reshape(*lengths[:dim], lengths[dim] * lengths[dim + 1], *lengths[dim + 2 :])


def sent_to_all(array, axis):
    copies = jnp.broadcast_to(array, (lax.axis_size(axis), *array.shape))
    return lax.all_to_all(copies, axis, split_axis=0, concat_axis=0, tiled=True)


def gather_directly(array, axis, dim):
    return joined_along(sent_to_all(array, axis), dim)


def passed_along(array, axis, by):
    devices = lax.axis_size(axis)
    pairs = [(i, i + by) for i in range(devices) if 0 <= i + by < devices]
    return lax.ppermute(array, axis, pairs)


def padded_2(cells, sides, width):
    for axis, dim in sides:
        count = lax.axis_size(axis)
        ends = count - 1
        head = lax.slice_in_dim(cells, 0, width, axis=dim)
        tail = lax.slice_in_dim(cells, cells.shape[dim] - width, cells.shape[dim], axis=dim)
        cells = jnp.concatenate(
            [
                lax.ppermute(tail, axis, [(i, (i + 1) % count) for i in range(ends)]),
                cells,
                lax.ppermute(head, axis, [((i + 1) % count, i) for i in range(ends)]),
            ],
            axis=dim,
        )
    return cells


def panels(whole):
    width = TILE + whole.shape[1]

    def skewed(values):
        padded = jnp.concatenate([values, jnp.zeros((TILE + 1,), values.dtype)])
        flat = jnp.tile(padded, TILE)[: TILE * width]
        return flat.reshape(TILE, width)

    return (skewed(whole[0]), skewed(whole[1]))


def compress(extended, offsets, panel_real, panel_imag, tiles):
    beams, pulses = (extended.shape[0], extended.shape[1])
    width = panel_real.shape[1]
    span = tiles * TILE + width - TILE

    def align(block, start):
        return lax.dynamic_slice_in_dim(block, start, span, 2)

    aligned = jax.vmap(align)(extended, offsets)
    rows = beams * pulses
    group = max(1, min(tiles, 256 // rows))
    while tiles % group:
        group = group - 1
    blocks = tiles // group
    dims = (((1,), (1,)), ((), ()))

    def block_fn(index):
        first = index * (group * TILE)
        windows = jnp.stack(
            [
                lax.dynamic_slice_in_dim(aligned, first + step * TILE, width, 3)
                for step in range(group)
            ]
        )
        real_part = windows[:, :, :, 0, :].reshape(group * rows, width)
        imag_part = windows[:, :, :, 1, :].reshape(group * rows, width)
        out_real = lax.dot_general(
            real_part, panel_real, dims, preferred_element_type=jnp.float32
        ) + lax.dot_general(imag_part, panel_imag, dims, preferred_element_type=jnp.float32)
        out_imag = lax.dot_general(
            imag_part, panel_real, dims, preferred_element_type=jnp.float32
        ) - lax.dot_general(real_part, panel_imag, dims, preferred_element_type=jnp.float32)
        return jnp.stack([out_real, out_imag], axis=1).reshape(group, beams, pulses, 2, TILE)

    outputs = lax.map(block_fn, jnp.arange(blocks, dtype=jnp.int32))
    outputs = outputs.reshape(tiles, beams, pulses, 2, TILE)
    return jnp.transpose(outputs, (1, 2, 3, 0, 4)).reshape(beams, pulses, 2, tiles * TILE)


def cell_power(compressed):
    real_part = compressed[:, :, 0].astype(jnp.float32)
    imag_part = compressed[:, :, 1].astype(jnp.float32)
    return real_part * real_part + imag_part * imag_part


def detect(padded, guard_cells, train_cells, scale_index, first_gate, total_gates):
    margin = GUARD_MAX + TRAIN_MAX
    beams, pulses = (padded.shape[0], padded.shape[1])
    length = padded.shape[2] - 2 * margin
    running = jnp.cumsum(padded, axis=2)
    prefix = jnp.concatenate([jnp.zeros((beams, pulses, 1), jnp.float32), running], axis=2)
    local = jnp.arange(length, dtype=jnp.int32)[None, :]
    guard = guard_cells[:, None]
    train = train_cells[:, None]

    def window(block, start):
        return lax.dynamic_slice_in_dim(block, start, length, 1)

    def pick(starts):
        return jax.vmap(window)(prefix, starts)

    lag = pick(margin - guard_cells) - pick(margin - guard_cells - train_cells)
    lead = pick(margin + guard_cells + train_cells + 1) - pick(margin + guard_cells + 1)
    position = first_gate + local
    count = jnp.clip(position - guard, 0, train) + jnp.clip(
        total_gates - 1 - position - guard, 0, train
    )
    noise = (lag + lead) / count.astype(jnp.float32)[:, None, :]
    factor = jnp.exp2(scale_index.astype(jnp.float32) / 8.0)
    power = padded[:, :, margin : margin + length]
    return power / (factor[:, None, None] * (noise + EPSILON))


def body(signal, replica, guard_cells, train_cells, scale_index, offsets):
    whole = gather_directly(replica, ("beam", "pulse"), 1)
    panel_real, panel_imag = panels(whole)
    gate_count = signal.shape[3]
    margin = GUARD_MAX + TRAIN_MAX
    needed = whole.shape[1] + OFF_MAX
    limit = min(-(-needed // gate_count), lax.axis_size("range") - 1)
    pieces = [signal]
    for step in range(1, limit + 1):
        keep = min(gate_count, needed - (step - 1) * gate_count)
        pieces.append(passed_along(signal[:, :, :, :keep], "range", -step))
    extended = jnp.concatenate(pieces, axis=3)
    compressed = compress(extended, offsets, panel_real, panel_imag, gate_count // TILE).astype(
        jnp.bfloat16
    )
    power = cell_power(compressed)
    padded = padded_2(power, (("range", 2),), margin)
    first_gate = lax.axis_index("range") * gate_count
    total_gates = gate_count * lax.axis_size("range")
    test_ratio = detect(padded, guard_cells, train_cells, scale_index, first_gate, total_gates)
    return (compressed, test_ratio)


def solution(mesh):
    placed = (
        P("beam", "pulse", None, "range"),
        P(None, ("beam", "pulse")),
        P("beam"),
        P("beam"),
        P("beam"),
        P("beam"),
    )
    return jax.shard_map(
        body,
        mesh=mesh,
        in_specs=placed,
        out_specs=(P("beam", "pulse", None, "range"), P("beam", "pulse", "range")),
        check_vma=False,
    )
```

profile of v0, /device:TPU:17, one launch (start us, length us, event | category | flops | bytes accessed | tf_op | source)
XLA Modules:
  0.0 79.5 jit_solution(2978307948528080120)
XLA Ops:
  0.6 1.3 %collective-permute-start.3 = (bf16[2,8,2,512]{3,2,1,0:T(2,128)(2,1)}, bf16[2,8,2,512]{3,2,1,0:T(2,128)(2,1)S(1)}, u32[]{:S(2)}, u32[]{:S(2)}) collective-permute-start(bf16[2,8,2,512]{3,2,1,0:T(2,128)(2,1)} %param.6), channel_id=1, source_target_pairs={{4,0},{5,1},{6,2},{7,3},{12,8},{13,9},{14,10},{15,11},{20,16},{21,... | collective-permute-start | bytes 98312 | tf_op jit(solution)/shard_map/ppermute | solution.py:33
  1.9 2.6 %collective-permute-start.2 = (bf16[2,8,2,512]{3,2,1,0:T(2,128)(2,1)}, bf16[2,8,2,512]{3,2,1,0:T(2,128)(2,1)S(1)}, u32[]{:S(2)}, u32[]{:S(2)}) collective-permute-start(bf16[2,8,2,512]{3,2,1,0:T(2,128)(2,1)} %param.6), channel_id=1, source_target_pairs={{3,0},{4,1},{5,2},{6,3},{7,4},{11,8},{12,9},{13,10},{14,11},{15,12... | collective-permute-start | bytes 98312 | tf_op jit(solution)/shard_map/ppermute | solution.py:33
  4.6 7.4 %collective-permute-start.1 = (bf16[2,8,2,512]{3,2,1,0:T(2,128)(2,1)}, bf16[2,8,2,512]{3,2,1,0:T(2,128)(2,1)S(1)}, u32[]{:S(2)}, u32[]{:S(2)}) collective-permute-start(bf16[2,8,2,512]{3,2,1,0:T(2,128)(2,1)} %param.6), channel_id=1, source_target_pairs={{2,0},{3,1},{4,2},{5,3},{6,4},{7,5},{10,8},{11,9},{12,10},{13,11},... | collective-permute-start | bytes 98312 | tf_op jit(solution)/shard_map/ppermute | solution.py:33
  12.0 2.7 %collective-permute-start = (bf16[2,8,2,512]{3,2,1,0:T(2,128)(2,1)}, bf16[2,8,2,512]{3,2,1,0:T(2,128)(2,1)S(1)}, u32[]{:S(2)}, u32[]{:S(2)}) collective-permute-start(bf16[2,8,2,512]{3,2,1,0:T(2,128)(2,1)} %param.6), channel_id=1, source_target_pairs={{1,0},{2,1},{3,2},{4,3},{5,4},{6,5},{7,6},{9,8},{10,9},{11,10},{12... | collective-permute-start | bytes 98312 | tf_op jit(solution)/shard_map/ppermute | solution.py:33
  14.7 0.7 slice.50
  15.4 1.3 %collective-permute-start.4 = (bf16[2,8,2,128]{3,2,1,0:T(2,128)(2,1)S(1)}, bf16[2,8,2,128]{3,2,1,0:T(2,128)(2,1)S(1)}, u32[]{:S(2)}, u32[]{:S(2)}) collective-permute-start(bf16[2,8,2,128]{3,2,1,0:T(2,128)(2,1)S(1)} %slice.50), channel_id=1, source_target_pairs={{5,0},{6,1},{7,2},{13,8},{14,9},{15,10},{21,16},{22,17},{23,18},{2... | collective-permute-start | bytes 24584 | tf_op jit(solution)/shard_map/ppermute | solution.py:33
  17.3 13.1 %all-to-all-start = ((bf16[64,2,32]{2,1,0:T(2,128)(2,1)}), bf16[64,2,32]{2,1,0:T(2,128)(2,1)S(1)}, u32[]{:S(2)}, u32[]{:S(2)}) async-start(bf16[64,2,32]{2,1,0:T(2,128)(2,1)} %broadcast_in_dim.28), calls=%async_computation | async-start | bytes 65536 | tf_op jit(solution)/shard_map/all_to_all | solution.py:23
  30.5 0.6 copy-done.4
  31.1 0.6 copy-done.1
  32.0 11.9 %all-to-all-done = bf16[64,2,32]{2,1,0:T(2,128)(2,1)S(1)} async-done(((bf16[64,2,32]{2,1,0:T(2,128)(2,1)}), bf16[64,2,32]{2,1,0:T(2,128)(2,1)S(1)}, u32[]{:S(2)}, u32[]{:S(2)}) %all-to-all-start) | async-done | bytes 8224 | tf_op jit(solution)/shard_map/all_to_all | solution.py:23
  44.4 0.7 tile.9
  45.8 0.7 tile.21
  47.4 4.1 %while.1 = (s32[]{:T(128)}, bf16[2,8,2,2688]{3,2,1,0:T(2,128)(2,1)S(1)}, s32[2,4]{1,0:T(2,128)S(1)}, bf16[2,8,2,2560]{3,1,0,2:T(8,128)(2,1)S(1)}, s32[]{:T(128)}) while((s32[]{:T(128)}, bf16[2,8,2,2688]{3,2,1,0:T(2,128)(2,1)S(1)}, s32[2,4]{1,0:T(2,128)S(1)}, bf16[2,8,2,2560]{3,1,0,2:T(8,128)(2,1)S(1)}, s32[]{:T(128)}) %tuple.43), condition=%wide.while_cond, body=%wide.while_body.sunk | while | flops 2 | bytes 327813 | solution.py:70
  48.1 1.4 %constant_dynamic-slice_fusion.5 = bf16[1,8,2,2560]{3,2,1,0:T(2,128)(2,1)S(1)} fusion(bf16[2,8,2,2688]{3,2,1,0:T(2,128)(2,1)S(1)} %get-tuple-element.115, s32[]{:T(128)} %bitcast.69, s32[]{:T(128)} %bitcast.70), kind=kLoop, calls=%fused_computation.6.clone.1 | loop fusion | bytes 163848 | tf_op jit(solution)/shard_map/vmap()/gather
  50.1 1.4 %constant_dynamic-slice_fusion.5 = bf16[1,8,2,2560]{3,2,1,0:T(2,128)(2,1)S(1)} fusion(bf16[2,8,2,2688]{3,2,1,0:T(2,128)(2,1)S(1)} %get-tuple-element.115, s32[]{:T(128)} %bitcast.69, s32[]{:T(128)} %bitcast.70), kind=kLoop, calls=%fused_computation.6.clone.1 | loop fusion | bytes 163848 | tf_op jit(solution)/shard_map/vmap()/gather
  53.2 5.1 %collective-permute-start.5 = (f32[2,8,104]{2,1,0:T(8,128)S(1)}, f32[2,8,104]{2,1,0:T(8,128)S(1)}, u32[]{:S(2)}, u32[]{:S(2)}) collective-permute-start(f32[2,8,104]{2,1,0:T(8,128)S(1)} %get-tuple-element.67), channel_id=1, source_target_pairs={{0,1},{1,2},{2,3},{3,4},{4,5},{5,6},{6,7},{8,9},{9,10},{10,11},{11... | collective-permute-start | bytes 19976 | tf_op jit(solution)/shard_map/ppermute | solution.py:44
  58.3 2.1 %collective-permute-start.6 = (f32[2,8,104]{2,1,0:T(8,128)S(1)}, f32[2,8,104]{2,1,0:T(8,128)S(1)}, u32[]{:S(2)}, u32[]{:S(2)}) collective-permute-start(f32[2,8,104]{2,1,0:T(8,128)S(1)} %get-tuple-element.68), channel_id=1, source_target_pairs={{1,0},{2,1},{3,2},{4,3},{5,4},{6,5},{7,6},{9,8},{10,9},{11,10},{12... | collective-permute-start | bytes 19976 | tf_op jit(solution)/shard_map/ppermute | solution.py:46
  61.1 2.2 %collective-permute-done.6 = f32[2,8,104]{2,1,0:T(8,128)S(1)} collective-permute-done((f32[2,8,104]{2,1,0:T(8,128)S(1)}, f32[2,8,104]{2,1,0:T(8,128)S(1)}, u32[]{:S(2)}, u32[]{:S(2)}) %collective-permute-start.6) | collective-permute-done | bytes 6688 | tf_op jit(solution)/shard_map/ppermute | solution.py:46
  63.4 3.4 %reduce-window.6 = f32[2,8,6,128]{3,1,2,0:T(8,128)S(1)} reduce-window(f32[2,8,6,128]{3,1,2,0:T(8,128)S(1)} %fusion.2, f32[]{:T(128)} %constant.71.clone.1), window={size=1x1x1x128 pad=0_0x0_0x0_0x127_0}, to_apply=%region_0.1 | reduce-window | flops 1560576 | bytes 98308 | tf_op jit(solution)/shard_map/reduce-window
  67.7 2.6 %gather_fusion.3 = f32[2,8,512]{1,0,2:T(2,128)S(1)} fusion(f32[2,8,721]{1,0,2:T(2,128)S(1)} %concatenate.37, s32[2]{0:T(128)S(1)} %get-tuple-element.72), kind=kCustom, calls=%fused_computation.3 | custom fusion | bytes 65560 | tf_op jit(solution)/shard_map/vmap()/gather | solution.py:120
  70.5 2.6 %gather_fusion.2 = f32[2,8,512]{1,0,2:T(2,128)S(1)} fusion(f32[2,8,721]{1,0,2:T(2,128)S(1)} %concatenate.37, s32[2]{0:T(128)S(1)} %get-tuple-element.70), kind=kCustom, calls=%fused_computation.2 | custom fusion | bytes 65560 | tf_op jit(solution)/shard_map/vmap()/gather | solution.py:120
  73.3 2.6 %gather_fusion.1 = f32[2,8,512]{1,0,2:T(2,128)S(1)} fusion(f32[2,8,721]{1,0,2:T(2,128)S(1)} %concatenate.37, s32[2]{0:T(128)S(1)} %get-tuple-element.69), kind=kCustom, calls=%fused_computation.1 | custom fusion | bytes 65560 | tf_op jit(solution)/shard_map/vmap()/gather | solution.py:120
  76.0 2.6 %gather_fusion = f32[2,8,512]{1,0,2:T(2,128)S(1)} fusion(f32[2,8,721]{1,0,2:T(2,128)S(1)} %concatenate.37, s32[2]{0:T(128)S(1)} %get-tuple-element.71), kind=kCustom, calls=%fused_computation | custom fusion | bytes 65560 | tf_op jit(solution)/shard_map/vmap()/gather | solution.py:120
  78.8 0.7 multiply_divide_fusion
  (73 shorter events, 7.9 us)
Async XLA Ops:
  0.6 16.1 %copy-start.3 = (bf16[2,32]{1,0:T(2,128)(2,1)S(1)}, bf16[2,32]{1,0:T(2,128)(2,1)}, u32[]{:S(2)}) copy-start(bf16[2,32]{1,0:T(2,128)(2,1)} %param.7) | copy-start | bytes 388
  0.6 46.7 %collective-permute-start.3 = (bf16[2,8,2,512]{3,2,1,0:T(2,128)(2,1)}, bf16[2,8,2,512]{3,2,1,0:T(2,128)(2,1)S(1)}, u32[]{:S(2)}, u32[]{:S(2)}) collective-permute-start(bf16[2,8,2,512]{3,2,1,0:T(2,128)(2,1)} %param.6), channel_id=1, source_target_pairs={{4,0},{5,1},{6,2},{7,3},{12,8},{13,9},{14,10},{15,11},{20,16},{21,... | collective-permute-start | bytes 98312 | tf_op jit(solution)/shard_map/ppermute | solution.py:33
  1.9 45.4 %collective-permute-start.2 = (bf16[2,8,2,512]{3,2,1,0:T(2,128)(2,1)}, bf16[2,8,2,512]{3,2,1,0:T(2,128)(2,1)S(1)}, u32[]{:S(2)}, u32[]{:S(2)}) collective-permute-start(bf16[2,8,2,512]{3,2,1,0:T(2,128)(2,1)} %param.6), channel_id=1, source_target_pairs={{3,0},{4,1},{5,2},{6,3},{7,4},{11,8},{12,9},{13,10},{14,11},{15,12... | collective-permute-start | bytes 98312 | tf_op jit(solution)/shard_map/ppermute | solution.py:33
  4.6 42.7 %collective-permute-start.1 = (bf16[2,8,2,512]{3,2,1,0:T(2,128)(2,1)}, bf16[2,8,2,512]{3,2,1,0:T(2,128)(2,1)S(1)}, u32[]{:S(2)}, u32[]{:S(2)}) collective-permute-start(bf16[2,8,2,512]{3,2,1,0:T(2,128)(2,1)} %param.6), channel_id=1, source_target_pairs={{2,0},{3,1},{4,2},{5,3},{6,4},{7,5},{10,8},{11,9},{12,10},{13,11},... | collective-permute-start | bytes 98312 | tf_op jit(solution)/shard_map/ppermute | solution.py:33
  12.0 35.2 %collective-permute-start = (bf16[2,8,2,512]{3,2,1,0:T(2,128)(2,1)}, bf16[2,8,2,512]{3,2,1,0:T(2,128)(2,1)S(1)}, u32[]{:S(2)}, u32[]{:S(2)}) collective-permute-start(bf16[2,8,2,512]{3,2,1,0:T(2,128)(2,1)} %param.6), channel_id=1, source_target_pairs={{1,0},{2,1},{3,2},{4,3},{5,4},{6,5},{7,6},{9,8},{10,9},{11,10},{12... | collective-permute-start | bytes 98312 | tf_op jit(solution)/shard_map/ppermute | solution.py:33
  15.4 32.0 %collective-permute-start.4 = (bf16[2,8,2,128]{3,2,1,0:T(2,128)(2,1)S(1)}, bf16[2,8,2,128]{3,2,1,0:T(2,128)(2,1)S(1)}, u32[]{:S(2)}, u32[]{:S(2)}) collective-permute-start(bf16[2,8,2,128]{3,2,1,0:T(2,128)(2,1)S(1)} %slice.50), channel_id=1, source_target_pairs={{5,0},{6,1},{7,2},{13,8},{14,9},{15,10},{21,16},{22,17},{23,18},{2... | collective-permute-start | bytes 24584 | tf_op jit(solution)/shard_map/ppermute | solution.py:33
  17.3 13.1 %copy-start = (bf16[2,8,2,512]{3,2,1,0:T(2,128)(2,1)S(1)}, bf16[2,8,2,512]{3,2,1,0:T(2,128)(2,1)}, u32[]{:S(2)}) copy-start(bf16[2,8,2,512]{3,2,1,0:T(2,128)(2,1)} %param.6) | copy-start | bytes 98308
  17.3 26.6 %all-to-all-start = ((bf16[64,2,32]{2,1,0:T(2,128)(2,1)}), bf16[64,2,32]{2,1,0:T(2,128)(2,1)S(1)}, u32[]{:S(2)}, u32[]{:S(2)}) async-start(bf16[64,2,32]{2,1,0:T(2,128)(2,1)} %broadcast_in_dim.28), calls=%async_computation | async-start | bytes 65536 | tf_op jit(solution)/shard_map/all_to_all | solution.py:23
  30.4 0.7 copy-start.4
  31.1 0.7 copy-start.1
  31.1 0.7 copy-start.2
  53.2 7.2 %copy-start.5 = (s32[2]{0:T(128)S(1)}, s32[2]{0:T(128)}, u32[]{:S(2)}) copy-start(s32[2]{0:T(128)} %param.10) | copy-start | bytes 28
  53.2 7.9 %collective-permute-start.5 = (f32[2,8,104]{2,1,0:T(8,128)S(1)}, f32[2,8,104]{2,1,0:T(8,128)S(1)}, u32[]{:S(2)}, u32[]{:S(2)}) collective-permute-start(f32[2,8,104]{2,1,0:T(8,128)S(1)} %get-tuple-element.67), channel_id=1, source_target_pairs={{0,1},{1,2},{2,3},{3,4},{4,5},{5,6},{6,7},{8,9},{9,10},{10,11},{11... | collective-permute-start | bytes 19976 | tf_op jit(solution)/shard_map/ppermute | solution.py:44
  58.3 5.0 %collective-permute-start.6 = (f32[2,8,104]{2,1,0:T(8,128)S(1)}, f32[2,8,104]{2,1,0:T(8,128)S(1)}, u32[]{:S(2)}, u32[]{:S(2)}) collective-permute-start(f32[2,8,104]{2,1,0:T(8,128)S(1)} %get-tuple-element.68), channel_id=1, source_target_pairs={{1,0},{2,1},{3,2},{4,3},{5,4},{6,5},{7,6},{9,8},{10,9},{11,10},{12... | collective-permute-start | bytes 19976 | tf_op jit(solution)/shard_map/ppermute | solution.py:46
where the time goes:
time: 80 us; the launch traced here: 79.5 us
  starting transfers between devices  35.6 us (44%)
  local copies, waits for them, and re-layouts  22.9 us (29%)
  waiting for transfers between devices  14.2 us (18%)
  other arithmetic  4.49 us (6%)
  matrix products  1.32 us (2%)
  between operations  1.03 us (1%)
    ppermute x5, starting transfers between devices, passed_along(): return lax.ppermute(array, axis, pairs)  15.3 us
    all_to_all x1, starting transfers between devices, sent_to_all(): return lax.all_to_all(copies, axis, split_axis=0, concat_axis=0, tiled=True)  13.1 us
    all_to_all x1, waiting for transfers between devices, sent_to_all(): return lax.all_to_all(copies, axis, split_axis=0, concat_axis=0, tiled=True)  11.9 us
    gather x8, local copies, waits for them, and re-layouts, window(): return lax.dynamic_slice_in_dim(block, start, length, 1)  11.1 us
    ppermute x1, starting transfers between devices, padded_2(): lax.ppermute(tail, axis, [(i, (i + 1) % count) for i in range(ends)])  5.1 us
    gather x8, local copies, waits for them, and re-layouts  4.07 us
    another operation x4, other arithmetic  3.57 us
    unnamed x21, local copies, waits for them, and re-layouts  2.53 us
  transfers between devices with their start and end apart: 8, of which 2 were waited for; matrix products, arithmetic and copies ran while one was open for 7% of the time, Pallas kernels for 0%

commit v1 on v0

v1 whole, which is shorter than its diff:
```python
import functools

import jax
import jax.numpy as jnp
from jax import lax
from jax.experimental import pallas as pl
from jax.experimental.pallas import tpu as pltpu
from jax.sharding import PartitionSpec as P


TILE = 128
EPSILON = 1e-6
INNER = 4
TILES = INNER + 2
CHUNKS = 17
BLOCKS = TILES + CHUNKS - 1


def sent_to_all(array, axis):
    copies = jnp.broadcast_to(array, (lax.axis_size(axis), *array.shape))
    return lax.all_to_all(copies, axis, split_axis=0, concat_axis=0, tiled=True)


def passed_along(array, axis, by):
    devices = lax.axis_size(axis)
    pairs = [(i, i + by) for i in range(devices) if 0 <= i + by < devices]
    return lax.ppermute(array, axis, pairs)


def prepare(shards, place_ref, guard_ref, train_ref, scale_ref, offset_ref, *refs):
    pieces, outs = refs[:-6], refs[-6:]
    left_ref, right_ref, window_ref, slope_ref, floor_ref, edge_ref = outs
    place = place_ref[0]
    lane = lax.broadcasted_iota(jnp.int32, (8, TILE), 1)
    blocks = [(ref, at) for ref in pieces for at in range(0, ref.shape[3], TILE)]

    aligned = []
    for beam in range(2):
        offset = offset_ref[beam]
        shift = lax.rem(TILE - offset, TILE)
        whole = lane < TILE - offset
        parts = []
        for part in range(2):
            rolled = [
                pltpu.roll(ref[beam, part, :, at : at + TILE].astype(jnp.float32), shift, 1)
                for ref, at in blocks
            ]
            parts.append([jnp.where(whole, rolled[n], rolled[n + 1]) for n in range(BLOCKS)])
        aligned.append(parts)
    for n in range(BLOCKS):
        real = jnp.concatenate([aligned[0][0][n], aligned[1][0][n]], axis=0)
        imag = jnp.concatenate([aligned[0][1][n], aligned[1][1][n]], axis=0)
        at = 2 * n * TILE
        left_ref[:, at : at + TILE] = real.astype(jnp.bfloat16)
        left_ref[:, at + TILE : at + 2 * TILE] = imag.astype(jnp.bfloat16)
        right_ref[:, at : at + TILE] = imag.astype(jnp.bfloat16)
        right_ref[:, at + TILE : at + 2 * TILE] = (-real).astype(jnp.bfloat16)

    apart = jnp.abs(
        lax.broadcasted_iota(jnp.int32, (3 * TILE, TILE), 0)
        - TILE
        - lax.broadcasted_iota(jnp.int32, (3 * TILE, TILE), 1)
    )
    gate = place * (INNER * TILE) + lax.broadcasted_iota(jnp.int32, (8, INNER * TILE), 1)
    last = shards * INNER * TILE - 1
    for beam in range(2):
        guard = guard_ref[beam]
        train = train_ref[beam]
        inside = jnp.logical_and(apart > guard, apart <= guard + train)
        window_ref[:, beam * TILE : (beam + 1) * TILE] = jnp.where(inside, 1.0, 0.0).astype(
            jnp.bfloat16
        )
        count = jnp.clip(gate - guard, 0, train) + jnp.clip(last - gate - guard, 0, train)
        level = jnp.full((8, TILE), scale_ref[beam], jnp.int32).astype(jnp.float32)
        factor = jnp.exp2(level / 8.0)
        slope_ref[8 * beam : 8 * beam + 8, :] = jnp.concatenate(
            [factor] * INNER, axis=1
        ) / count.astype(jnp.float32)
        floor_ref[8 * beam : 8 * beam + 8, :] = factor * EPSILON
    edge_ref[0:8, :] = jnp.where(jnp.full((8, TILE), place, jnp.int32) > 0, 1.0, 0.0)
    edge_ref[8:16, :] = jnp.where(jnp.full((8, TILE), place, jnp.int32) < shards - 1, 1.0, 0.0)


def detect(taps_ref, left_ref, right_ref, window_ref, slope_ref, floor_ref, edge_ref, *outs):
    compressed_ref, ratio_ref = outs
    across = (((1,), (1,)), ((), ()))
    lane = lax.broadcasted_iota(jnp.int32, (8, TILE), 1)
    row = lax.broadcasted_iota(jnp.int32, (8, TILE), 0)

    rows = []
    for part in range(2):
        quarters = [taps_ref[pl.ds(2 * q + part, 16, stride=8), :] for q in range(4)]
        rows.append(jnp.concatenate(quarters, axis=1))

    total = jnp.zeros((2 * TILES * 16, TILE), jnp.float32)
    before = None
    for chunk in range(CHUNKS):
        rolled = []
        for part in range(2):
            if chunk < CHUNKS - 1:
                line = jnp.broadcast_to(rows[part][chunk : chunk + 1, :], (8, TILE))
                rolled.append(
                    [pltpu.roll(line, 8 * q, 1, stride=1, stride_axis=0) for q in range(16)]
                )
            else:
                rolled.append([jnp.zeros((8, TILE), jnp.float32)] * 16)
        panel = []
        for part in range(2):
            pieces = []
            for q in range(16):
                old = before[part][q] if before is not None else jnp.zeros((8, TILE), jnp.float32)
                pieces.append(jnp.where(lane >= 8 * q + row, rolled[part][q], old))
            panel.append(jnp.concatenate(pieces, axis=0).astype(jnp.bfloat16))
        before = rolled
        weights = jnp.concatenate(panel, axis=1)
        samples = [
            ref[:, 2 * (tile + chunk) * TILE : 2 * (tile + chunk + 1) * TILE]
            for ref in (left_ref, right_ref)
            for tile in range(TILES)
        ]
        total = total + lax.dot_general(
            jnp.concatenate(samples, axis=0), weights, across, preferred_element_type=jnp.float32
        )

    rounded = total.astype(jnp.bfloat16)
    half = TILES * 16
    power = []
    for tile in range(TILES):
        real = rounded[16 * tile : 16 * tile + 16]
        imag = rounded[half + 16 * tile : half + 16 * tile + 16]
        if 1 <= tile <= INNER:
            at = (tile - 1) * TILE
            for beam in range(2):
                compressed_ref[beam, 0, :, at : at + TILE] = real[8 * beam : 8 * beam + 8]
                compressed_ref[beam, 1, :, at : at + TILE] = imag[8 * beam : 8 * beam + 8]
        real = real.astype(jnp.float32)
        imag = imag.astype(jnp.float32)
        power.append(real * real + imag * imag)
    power[0] = power[0] * jnp.concatenate([edge_ref[0:8, :]] * 2, axis=0)
    power[-1] = power[-1] * jnp.concatenate([edge_ref[8:16, :]] * 2, axis=0)

    terms = []
    rest = power
    for _ in range(3):
        term = [cells.astype(jnp.bfloat16) for cells in rest]
        rest = [cells - t.astype(jnp.float32) for cells, t in zip(rest, term)]
        terms += [
            jnp.concatenate(term[tile - 1 : tile + 2], axis=1) for tile in range(1, INNER + 1)
        ]
    sums = lax.dot_general(
        jnp.concatenate(terms, axis=0),
        window_ref[...],
        (((1,), (0,)), ((), ())),
        preferred_element_type=jnp.float32,
    )
    size = INNER * 16
    sums = sums[2 * size :] + sums[size : 2 * size] + sums[:size]
    for tile in range(INNER):
        at = tile * TILE
        for beam in range(2):
            noise = sums[16 * tile + 8 * beam : 16 * tile + 8 * beam + 8]
            noise = noise[:, beam * TILE : (beam + 1) * TILE]
            rows_of = slice(8 * beam, 8 * beam + 8)
            ratio_ref[beam, :, at : at + TILE] = power[tile + 1][rows_of] / (
                noise * slope_ref[rows_of, at : at + TILE] + floor_ref[rows_of, :]
            )


def body(signal, replica, guard_cells, train_cells, scale_index, offsets):
    shards = lax.axis_size("range")
    vmem = pl.BlockSpec(memory_space=pltpu.VMEM)
    smem = pl.BlockSpec(memory_space=pltpu.SMEM)
    f32, bf16 = jnp.float32, jnp.bfloat16

    taps = sent_to_all(replica.astype(f32), ("beam", "pulse"))
    cells = jnp.transpose(signal, (0, 2, 1, 3))
    own = cells.shape[3]
    pieces = [passed_along(cells[..., own - TILE :], "range", 1), cells]
    pieces += [passed_along(cells, "range", -step) for step in range(1, 5)]
    pieces.append(passed_along(cells[..., : 2 * TILE], "range", -5))
    taps = taps.reshape(-1, taps.shape[-1])
    place = lax.axis_index("range").reshape(1)
    prepared = pl.pallas_call(
        functools.partial(prepare, shards),
        out_shape=(
            jax.ShapeDtypeStruct((16, 2 * BLOCKS * TILE), bf16),
            jax.ShapeDtypeStruct((16, 2 * BLOCKS * TILE), bf16),
            jax.ShapeDtypeStruct((3 * TILE, 2 * TILE), bf16),
            jax.ShapeDtypeStruct((16, INNER * TILE), f32),
            jax.ShapeDtypeStruct((16, TILE), f32),
            jax.ShapeDtypeStruct((16, TILE), f32),
        ),
        in_specs=[smem] * 5 + [vmem] * len(pieces),
        out_specs=[vmem] * 6,
        compiler_params=pltpu.CompilerParams(vmem_limit_bytes=4 << 20),
        cost_estimate=pl.CostEstimate(flops=1 << 20, bytes_accessed=1 << 20, transcendentals=0),
        name="prepare",
    )(place, guard_cells, train_cells, scale_index, offsets, *pieces)
    compressed, ratio = pl.pallas_call(
        detect,
        out_shape=(
            jax.ShapeDtypeStruct((2, 2, 8, INNER * TILE), bf16),
            jax.ShapeDtypeStruct((2, 8, INNER * TILE), f32),
        ),
        in_specs=[vmem] * 7,
        out_specs=[vmem] * 2,
        compiler_params=pltpu.CompilerParams(vmem_limit_bytes=4 << 20),
        cost_estimate=pl.CostEstimate(flops=1 << 28, bytes_accessed=1 << 20, transcendentals=0),
        name="detect",
    )(taps, *prepared)
    return jnp.transpose(compressed, (0, 2, 1, 3)), ratio


def solution(mesh):
    placed = (
        P("beam", "pulse", None, "range"),
        P(None, ("beam", "pulse")),
        P("beam"),
        P("beam"),
        P("beam"),
        P("beam"),
    )
    return jax.shard_map(
        body,
        mesh=mesh,
        in_specs=placed,
        out_specs=(P("beam", "pulse", None, "range"), P("beam", "pulse", "range")),
        check_vma=False,
    )
```

time: 80 us -> 44.5 us (0.56)
  the two profiles are of different devices: /device:TPU:17 before, /device:TPU:1 now
where the time goes in v1:
time: 44.5 us; the launch traced here: 44.2 us
  starting transfers between devices  31 us (70%)
  waiting for transfers between devices  7.95 us (18%)
  Pallas kernels  2.45 us (6%)
  local copies, waits for them, and re-layouts  1.97 us (4%)
  between operations  0.81 us (2%)
    all_to_all x1, starting transfers between devices, sent_to_all(): return lax.all_to_all(copies, axis, split_axis=0, concat_axis=0, tiled=True)  19.2 us
    ppermute x6, starting transfers between devices, passed_along(): return lax.ppermute(array, axis, pairs)  11.8 us
    ppermute x6, waiting for transfers between devices, passed_along(): return lax.ppermute(array, axis, pairs)  7.95 us
    pallas_call x1, Pallas kernels, body(): pl.pallas_call(detect, out_shape=(jax.ShapeDtypeStruct((2, 2, 8, INNER *...  1.69 us
    broadcast_in_dim x1, local copies, waits for them, and re-layouts, sent_to_all(): copies = jnp.broadcast_to(array, (lax.axis_size(axis), *array.shape))  1.29 us
  transfers between devices with their start and end apart: 7, of which 2 were waited for; matrix products, arithmetic and copies ran while one was open for 0% of the time, Pallas kernels for 2%

profile of v1, /device:TPU:1, one launch (start us, length us, event | category | flops | bytes accessed | tf_op | source)
XLA Modules:
  0.0 44.2 jit_solution(16690161841317739137)
XLA Ops:
  0.6 1.3 %broadcast_in_dim.3 = f32[64,2,32]{2,1,0:T(2,128)} broadcast(bf16[2,32]{1,0:T(2,128)(2,1)} %param.7), dimensions={1,2} | broadcast | bytes 16512 | tf_op jit(solution)/shard_map/broadcast_in_dim | solution.py:20
  1.9 19.2 %all-to-all-start = ((f32[64,2,32]{2,1,0:T(2,128)}), f32[64,2,32]{2,1,0:T(2,128)S(1)}, u32[]{:S(2)}, u32[]{:S(2)}) async-start(f32[64,2,32]{2,1,0:T(2,128)} %broadcast_in_dim.3), calls=%async_computation | async-start | bytes 131072 | tf_op jit(solution)/shard_map/all_to_all | solution.py:21
  21.2 0.0 copy-done.4
  21.2 2.9 %collective-permute-start.1 = (bf16[2,2,8,512]{3,2,1,0:T(8,128)(2,1)S(1)}, bf16[2,2,8,512]{3,2,1,0:T(8,128)(2,1)S(1)}, u32[]{:S(2)}, u32[]{:S(2)}) collective-permute-start(bf16[2,2,8,512]{3,2,1,0:T(8,128)(2,1)S(1)} %bitcast.6), channel_id=1, source_target_pairs={{1,0},{2,1},{3,2},{4,3},{5,4},{6,5},{7,6},{9,8},{10,9},{11,10},{12... | collective-permute-start | bytes 98312 | tf_op jit(solution)/shard_map/ppermute | solution.py:27
  24.1 1.3 %collective-permute-start.2 = (bf16[2,2,8,512]{3,2,1,0:T(8,128)(2,1)S(1)}, bf16[2,2,8,512]{3,2,1,0:T(8,128)(2,1)S(1)}, u32[]{:S(2)}, u32[]{:S(2)}) collective-permute-start(bf16[2,2,8,512]{3,2,1,0:T(8,128)(2,1)S(1)} %bitcast.7), channel_id=1, source_target_pairs={{2,0},{3,1},{4,2},{5,3},{6,4},{7,5},{10,8},{11,9},{12,10},{13,11},... | collective-permute-start | bytes 98312 | tf_op jit(solution)/shard_map/ppermute | solution.py:27
  25.4 1.3 %collective-permute-start.3 = (bf16[2,2,8,512]{3,2,1,0:T(8,128)(2,1)S(1)}, bf16[2,2,8,512]{3,2,1,0:T(8,128)(2,1)S(1)}, u32[]{:S(2)}, u32[]{:S(2)}) collective-permute-start(bf16[2,2,8,512]{3,2,1,0:T(8,128)(2,1)S(1)} %bitcast.8), channel_id=1, source_target_pairs={{3,0},{4,1},{5,2},{6,3},{7,4},{11,8},{12,9},{13,10},{14,11},{15,12... | collective-permute-start | bytes 98312 | tf_op jit(solution)/shard_map/ppermute | solution.py:27
  26.7 1.3 %collective-permute-start.4 = (bf16[2,2,8,512]{3,2,1,0:T(8,128)(2,1)S(1)}, bf16[2,2,8,512]{3,2,1,0:T(8,128)(2,1)S(1)}, u32[]{:S(2)}, u32[]{:S(2)}) collective-permute-start(bf16[2,2,8,512]{3,2,1,0:T(8,128)(2,1)S(1)} %bitcast.9), channel_id=1, source_target_pairs={{4,0},{5,1},{6,2},{7,3},{12,8},{13,9},{14,10},{15,11},{20,16},{21,... | collective-permute-start | bytes 98312 | tf_op jit(solution)/shard_map/ppermute | solution.py:27
  28.0 3.7 %collective-permute-start = (bf16[2,2,8,128]{3,2,1,0:T(8,128)(2,1)S(1)}, bf16[2,2,8,128]{3,2,1,0:T(8,128)(2,1)S(1)}, u32[]{:S(2)}, u32[]{:S(2)}) collective-permute-start(bf16[2,2,8,128]{3,2,1,0:T(8,128)(2,1)S(1)} %slice.8), channel_id=1, source_target_pairs={{0,1},{1,2},{2,3},{3,4},{4,5},{5,6},{6,7},{8,9},{9,10},{10,11},{11... | collective-permute-start | bytes 24584 | tf_op jit(solution)/shard_map/ppermute | solution.py:27
  31.7 0.8 %collective-permute-done.refs_0_ = bf16[2,2,8,128]{3,2,1,0:T(8,128)(2,1)S(1)} collective-permute-done((bf16[2,2,8,128]{3,2,1,0:T(8,128)(2,1)S(1)}, bf16[2,2,8,128]{3,2,1,0:T(8,128)(2,1)S(1)}, u32[]{:S(2)}, u32[]{:S(2)}) %collective-permute-start) | collective-permute-done | bytes 8224 | tf_op jit(solution)/shard_map/ppermute | solution.py:27
  32.5 1.3 %collective-permute-start.5 = (bf16[2,2,8,256]{3,2,1,0:T(8,128)(2,1)S(1)}, bf16[2,2,8,256]{3,2,1,0:T(8,128)(2,1)S(1)}, u32[]{:S(2)}, u32[]{:S(2)}) collective-permute-start(bf16[2,2,8,256]{3,2,1,0:T(8,128)(2,1)S(1)} %slice.9), channel_id=1, source_target_pairs={{5,0},{6,1},{7,2},{13,8},{14,9},{15,10},{21,16},{22,17},{23,18},{2... | collective-permute-start | bytes 49160 | tf_op jit(solution)/shard_map/ppermute | solution.py:27
  33.8 0.0 copy-start.3
  33.8 0.0 copy-start
  33.8 0.0 copy-start.1
  33.8 0.0 copy-start.2
  33.8 7.2 %collective-permute-done.5.refs_6_ = bf16[2,2,8,256]{3,2,1,0:T(8,128)(2,1)S(1)} collective-permute-done((bf16[2,2,8,256]{3,2,1,0:T(8,128)(2,1)S(1)}, bf16[2,2,8,256]{3,2,1,0:T(8,128)(2,1)S(1)}, u32[]{:S(2)}, u32[]{:S(2)}) %collective-permute-start.5) | collective-permute-done | bytes 16416 | tf_op jit(solution)/shard_map/ppermute | solution.py:27
  41.0 0.0 collective-permute-done.1.refs_2_
  41.0 0.0 collective-permute-done.2.refs_3_
  41.0 0.0 collective-permute-done.3.refs_4_
  41.0 0.0 collective-permute-done.4.refs_5_
  41.0 0.0 copy-done.3
  41.1 0.8 %prepare.1 = (bf16[16,5632]{1,0:T(8,128)(2,1)S(1)}, bf16[16,5632]{1,0:T(8,128)(2,1)S(1)}, bf16[384,256]{1,0:T(8,128)(2,1)S(1)}, f32[16,512]{1,0:T(8,128)S(1)}, f...) custom-call(s32[1]{0:T(128)} %bitcast.1.place_ref, s32[2]{0:T(128)S(1)} %copy-done, s32[2]{0:T(128)S(1)} %copy-done.1, ...), custom_call_target="tpu_custom_call" | custom-call | flops 1048576 | bytes 1048576 | tf_op jit(solution)/shard_map/prepare/pallas_call | solution.py:183
  41.8 0.0 all-to-all-done
  41.8 1.7 %detect.1 = (bf16[2,2,8,512]{3,2,1,0:T(8,128)(2,1)S(1)}, f32[2,8,512]{2,1,0:T(8,128)}) custom-call(f32[128,32]{1,0:T(8,128)S(1)} %bitcast.13, bf16[16,5632]{1,0:T(8,128)(2,1)S(1)} %get-tuple-element.10.left_ref, bf16[16,5632]{1,0:T(8,128)(2,1)S(1)} %get-tuple-element.11.right_ref, bf16[384,256]{1,0:T(8,128)(2,1)S(1)} %get-tuple-element.12.window_ref, ...), custom_call_target="tpu_custom_call" | custom-call | flops 268435456 | bytes 1048576 | tf_op jit(solution)/shard_map/detect/pallas_call | solution.py:199
  43.5 0.6 %copy.9 = bf16[2,8,2,512]{3,2,1,0:T(2,128)(2,1)} copy(bf16[2,8,2,512]{3,1,2,0:T(8,128)(2,1)S(1)} %bitcast.14) | data formatting | bytes 65536
  (7 shorter events, 0.0 us)
Async XLA Ops:
  1.9 19.2 %copy-start.4 = (bf16[2,8,2,512]{3,2,1,0:T(2,128)(2,1)S(1)}, bf16[2,8,2,512]{3,2,1,0:T(2,128)(2,1)}, u32[]{:S(2)}) copy-start(bf16[2,8,2,512]{3,2,1,0:T(2,128)(2,1)} %param.6) | copy-start | bytes 98308
  1.9 39.9 %all-to-all-start = ((f32[64,2,32]{2,1,0:T(2,128)}), f32[64,2,32]{2,1,0:T(2,128)S(1)}, u32[]{:S(2)}, u32[]{:S(2)}) async-start(f32[64,2,32]{2,1,0:T(2,128)} %broadcast_in_dim.3), calls=%async_computation | async-start | bytes 131072 | tf_op jit(solution)/shard_map/all_to_all | solution.py:21
  21.2 19.8 %collective-permute-start.1 = (bf16[2,2,8,512]{3,2,1,0:T(8,128)(2,1)S(1)}, bf16[2,2,8,512]{3,2,1,0:T(8,128)(2,1)S(1)}, u32[]{:S(2)}, u32[]{:S(2)}) collective-permute-start(bf16[2,2,8,512]{3,2,1,0:T(8,128)(2,1)S(1)} %bitcast.6), channel_id=1, source_target_pairs={{1,0},{2,1},{3,2},{4,3},{5,4},{6,5},{7,6},{9,8},{10,9},{11,10},{12... | collective-permute-start | bytes 98312 | tf_op jit(solution)/shard_map/ppermute | solution.py:27
  24.1 16.9 %collective-permute-start.2 = (bf16[2,2,8,512]{3,2,1,0:T(8,128)(2,1)S(1)}, bf16[2,2,8,512]{3,2,1,0:T(8,128)(2,1)S(1)}, u32[]{:S(2)}, u32[]{:S(2)}) collective-permute-start(bf16[2,2,8,512]{3,2,1,0:T(8,128)(2,1)S(1)} %bitcast.7), channel_id=1, source_target_pairs={{2,0},{3,1},{4,2},{5,3},{6,4},{7,5},{10,8},{11,9},{12,10},{13,11},... | collective-permute-start | bytes 98312 | tf_op jit(solution)/shard_map/ppermute | solution.py:27
  25.4 15.6 %collective-permute-start.3 = (bf16[2,2,8,512]{3,2,1,0:T(8,128)(2,1)S(1)}, bf16[2,2,8,512]{3,2,1,0:T(8,128)(2,1)S(1)}, u32[]{:S(2)}, u32[]{:S(2)}) collective-permute-start(bf16[2,2,8,512]{3,2,1,0:T(8,128)(2,1)S(1)} %bitcast.8), channel_id=1, source_target_pairs={{3,0},{4,1},{5,2},{6,3},{7,4},{11,8},{12,9},{13,10},{14,11},{15,12... | collective-permute-start | bytes 98312 | tf_op jit(solution)/shard_map/ppermute | solution.py:27
  26.7 14.4 %collective-permute-start.4 = (bf16[2,2,8,512]{3,2,1,0:T(8,128)(2,1)S(1)}, bf16[2,2,8,512]{3,2,1,0:T(8,128)(2,1)S(1)}, u32[]{:S(2)}, u32[]{:S(2)}) collective-permute-start(bf16[2,2,8,512]{3,2,1,0:T(8,128)(2,1)S(1)} %bitcast.9), channel_id=1, source_target_pairs={{4,0},{5,1},{6,2},{7,3},{12,8},{13,9},{14,10},{15,11},{20,16},{21,... | collective-permute-start | bytes 98312 | tf_op jit(solution)/shard_map/ppermute | solution.py:27
  28.0 4.5 %collective-permute-start = (bf16[2,2,8,128]{3,2,1,0:T(8,128)(2,1)S(1)}, bf16[2,2,8,128]{3,2,1,0:T(8,128)(2,1)S(1)}, u32[]{:S(2)}, u32[]{:S(2)}) collective-permute-start(bf16[2,2,8,128]{3,2,1,0:T(8,128)(2,1)S(1)} %slice.8), channel_id=1, source_target_pairs={{0,1},{1,2},{2,3},{3,4},{4,5},{5,6},{6,7},{8,9},{9,10},{10,11},{11... | collective-permute-start | bytes 24584 | tf_op jit(solution)/shard_map/ppermute | solution.py:27
  32.5 8.5 %collective-permute-start.5 = (bf16[2,2,8,256]{3,2,1,0:T(8,128)(2,1)S(1)}, bf16[2,2,8,256]{3,2,1,0:T(8,128)(2,1)S(1)}, u32[]{:S(2)}, u32[]{:S(2)}) collective-permute-start(bf16[2,2,8,256]{3,2,1,0:T(8,128)(2,1)S(1)} %slice.9), channel_id=1, source_target_pairs={{5,0},{6,1},{7,2},{13,8},{14,9},{15,10},{21,16},{22,17},{23,18},{2... | collective-permute-start | bytes 49160 | tf_op jit(solution)/shard_map/ppermute | solution.py:27
  33.8 7.2 %copy-start.3 = (s32[2]{0:T(128)S(1)}, s32[2]{0:T(128)}, u32[]{:S(2)}) copy-start(s32[2]{0:T(128)} %offset_ref.1) | copy-start | bytes 28
  33.8 7.2 %copy-start = (s32[2]{0:T(128)S(1)}, s32[2]{0:T(128)}, u32[]{:S(2)}) copy-start(s32[2]{0:T(128)} %guard_ref.1) | copy-start | bytes 28
  33.8 7.2 %copy-start.1 = (s32[2]{0:T(128)S(1)}, s32[2]{0:T(128)}, u32[]{:S(2)}) copy-start(s32[2]{0:T(128)} %train_ref.1) | copy-start | bytes 28
  33.8 7.2 %copy-start.2 = (s32[2]{0:T(128)S(1)}, s32[2]{0:T(128)}, u32[]{:S(2)}) copy-start(s32[2]{0:T(128)} %scale_ref.1) | copy-start | bytes 28

commit v2 on v1

--- a/solution.py
+++ b/solution.py
@@ -21,18 +21,41 @@
     return lax.all_to_all(copies, axis, split_axis=0, concat_axis=0, tiled=True)
 
 
-def passed_along(array, axis, by):
-    devices = lax.axis_size(axis)
-    pairs = [(i, i + by) for i in range(devices) if 0 <= i + by < devices]
-    return lax.ppermute(array, axis, pairs)
+def strip_of_chip(signal):
+    devices = lax.axis_size("range")
+    cells = jnp.transpose(signal, (0, 2, 1, 3))
+    half = cells.shape[3] // 2
+    own = jnp.stack([cells[..., :half], cells[..., half:]])
+
+    def sent(array, pairs):
+        inside = [(i, j) for i, j in pairs if 0 <= i < devices]
+        return lax.ppermute(array, "range", inside)
+
+    first = lax.rem(lax.axis_index("range"), 2) == 0
+    ends = [(j + 6 if j % 2 == 0 else j - 2, j) for j in range(devices)]
+    ahead = sent(own, [(j + 2, j) for j in range(devices)])
+    farther = sent(own, [(j + 4, j) for j in range(devices)])
+    rest = sent(jnp.where(first, own[:1], own[1:]), ends)
+    mine = jnp.concatenate([own, ahead, farther, rest], axis=0)
+    chips = [[2 * i, 2 * i + 1] for i in range(devices // 2)]
+    return lax.all_gather(mine, "range", axis_index_groups=chips, tiled=True)
 
 
 def prepare(shards, place_ref, guard_ref, train_ref, scale_ref, offset_ref, *refs):
-    pieces, outs = refs[:-6], refs[-6:]
+    strip_ref, outs = refs[0], refs[1:]
     left_ref, right_ref, window_ref, slope_ref, floor_ref, edge_ref = outs
     place = place_ref[0]
     lane = lax.broadcasted_iota(jnp.int32, (8, TILE), 1)
-    blocks = [(ref, at) for ref in pieces for at in range(0, ref.shape[3], TILE)]
+
+    count = strip_ref.shape[0] // 2
+    strip = [2 * count - 1]
+    strip += [core * count + at + sub for at in (0, 2, 4) for core in (0, 1) for sub in (0, 1)]
+    strip += [count - 1]
+    core = lax.rem(place, 2)
+    blocks = []
+    for n in range(len(strip) - 2):
+        piece = jnp.where(core == 0, strip[n], strip[n + 2])
+        blocks += [(piece, at) for at in ((TILE,) if n == 0 else (0, TILE))]
 
     aligned = []
     for beam in range(2):
@@ -42,8 +65,10 @@
         parts = []
         for part in range(2):
             rolled = [
-                pltpu.roll(ref[beam, part, :, at : at + TILE].astype(jnp.float32), shift, 1)
-                for ref, at in blocks
+                pltpu.roll(
+                    strip_ref[piece, beam, part, :, at : at + TILE].astype(jnp.float32), shift, 1
+                )
+                for piece, at in blocks
             ]
             parts.append([jnp.where(whole, rolled[n], rolled[n + 1]) for n in range(BLOCKS)])
         aligned.append(parts)
@@ -173,11 +198,7 @@
     f32, bf16 = jnp.float32, jnp.bfloat16
 
     taps = sent_to_all(replica.astype(f32), ("beam", "pulse"))
-    cells = jnp.transpose(signal, (0, 2, 1, 3))
-    own = cells.shape[3]
-    pieces = [passed_along(cells[..., own - TILE :], "range", 1), cells]
-    pieces += [passed_along(cells, "range", -step) for step in range(1, 5)]
-    pieces.append(passed_along(cells[..., : 2 * TILE], "range", -5))
+    strip = strip_of_chip(signal)
     taps = taps.reshape(-1, taps.shape[-1])
     place = lax.axis_index("range").reshape(1)
     prepared = pl.pallas_call(
@@ -190,12 +211,12 @@
             jax.ShapeDtypeStruct((16, TILE), f32),
             jax.ShapeDtypeStruct((16, TILE), f32),
         ),
-        in_specs=[smem] * 5 + [vmem] * len(pieces),
+        in_specs=[smem] * 5 + [vmem],
         out_specs=[vmem] * 6,
         compiler_params=pltpu.CompilerParams(vmem_limit_bytes=4 << 20),
         cost_estimate=pl.CostEstimate(flops=1 << 20, bytes_accessed=1 << 20, transcendentals=0),
         name="prepare",
-    )(place, guard_cells, train_cells, scale_index, offsets, *pieces)
+    )(place, guard_cells, train_cells, scale_index, offsets, strip)
     compressed, ratio = pl.pallas_call(
         detect,
         out_shape=(

time: 44.5 us -> 45.3 us (1.018)
  the two profiles are of different devices: /device:TPU:1 before, /device:TPU:24 now
where the time goes in v2:
time: 45.3 us; the launch traced here: 45 us
  starting transfers between devices  25.3 us (56%)
  waiting for transfers between devices  11.7 us (26%)
  local copies, waits for them, and re-layouts  2.77 us (6%)
  Pallas kernels  2.42 us (5%)
  blocking collectives  1.97 us (4%)
  between operations  0.78 us (2%)
    all_to_all x1, starting transfers between devices, sent_to_all(): return lax.all_to_all(copies, axis, split_axis=0, concat_axis=0, tiled=True)  13.2 us
    ppermute x3, starting transfers between devices, sent(): return lax.ppermute(array, 'range', inside)  12.1 us
    all_to_all x1, waiting for transfers between devices, sent_to_all(): return lax.all_to_all(copies, axis, split_axis=0, concat_axis=0, tiled=True)  11.7 us
    unnamed x16, local copies, waits for them, and re-layouts  2.11 us
    all_gather x1, blocking collectives, strip_of_chip(): return lax.all_gather(mine, 'range', axis_index_groups=chips, tiled=True)  1.97 us
    pallas_call x1, Pallas kernels, body(): pl.pallas_call(detect, out_shape=(jax.ShapeDtypeStruct((2, 2, 8, INNER *...  1.67 us
  transfers between devices with their start and end apart: 4, of which 1 were waited for; matrix products, arithmetic and copies ran while one was open for 1% of the time, Pallas kernels for 2%

profile of v2, /device:TPU:24, one launch (start us, length us, event | category | flops | bytes accessed | tf_op | source)
XLA Modules:
  0.0 45.0 jit_solution(8401279381890397835)
XLA Ops:
  0.6 0.8 %copy.13 = bf16[2,8,2,512]{3,1,2,0:T(8,128)(2,1)S(1)} copy(bf16[2,8,2,512]{3,2,1,0:T(2,128)(2,1)} %param.6) | data formatting | bytes 65536 | tf_op args[0]
  1.4 0.0 copy-start.4
  1.4 2.6 %collective-permute-start = (bf16[2,2,2,8,256]{4,3,2,1,0:T(8,128)(2,1)S(1)}, bf16[2,2,2,8,256]{4,3,2,1,0:T(8,128)(2,1)S(1)}, u32[]{:S(2)}, u32[]{:S(2)}) collective-permute-start(bf16[2,2,2,8,256]{4,3,2,1,0:T(8,128)(2,1)S(1)} %pad_maximum_fusion), channel_id=1, source_target_pairs={{2,0},{3,1},{4,2},{5,3},{6,4},{7,5},{10,8},{11,9},{12,10},{13,11},... | collective-permute-start | bytes 98312 | tf_op jit(solution)/shard_map/ppermute | solution.py:32
  4.1 8.2 %collective-permute-start.1 = (bf16[2,2,2,8,256]{4,3,2,1,0:T(8,128)(2,1)S(1)}, bf16[2,2,2,8,256]{4,3,2,1,0:T(8,128)(2,1)S(1)}, u32[]{:S(2)}, u32[]{:S(2)}) collective-permute-start(bf16[2,2,2,8,256]{4,3,2,1,0:T(8,128)(2,1)S(1)} %pad_maximum_fusion), channel_id=1, source_target_pairs={{4,0},{5,1},{6,2},{7,3},{12,8},{13,9},{14,10},{15,11},{20,16},{21,... | collective-permute-start | bytes 98312 | tf_op jit(solution)/shard_map/ppermute | solution.py:32
  12.3 1.3 %collective-permute-start.2 = (bf16[1,2,2,8,256]{4,3,2,1,0:T(8,128)(2,1)S(1)}, bf16[1,2,2,8,256]{4,3,2,1,0:T(8,128)(2,1)S(1)}, u32[]{:S(2)}, u32[]{:S(2)}) collective-permute-start(bf16[1,2,2,8,256]{4,3,2,1,0:T(8,128)(2,1)S(1)} %get-tuple-element.22), channel_id=1, source_target_pairs={{6,0},{1,3},{3,5},{5,7},{14,8},{9,11},{11,13},{13,15},{22,16},{17,... | collective-permute-start | bytes 49160 | tf_op jit(solution)/shard_map/ppermute | solution.py:32
  13.6 0.0 copy-done.4
  13.6 0.7 %broadcast_in_dim.3 = f32[64,2,32]{2,1,0:T(2,128)} broadcast(bf16[2,32]{1,0:T(2,128)(2,1)S(1)} %copy-done.4), dimensions={1,2} | broadcast | bytes 16512 | tf_op jit(solution)/shard_map/broadcast_in_dim | solution.py:20
  14.3 13.2 %all-to-all-start = ((f32[64,2,32]{2,1,0:T(2,128)}), f32[64,2,32]{2,1,0:T(2,128)S(1)}, u32[]{:S(2)}, u32[]{:S(2)}) async-start(f32[64,2,32]{2,1,0:T(2,128)} %broadcast_in_dim.3), calls=%async_computation | async-start | bytes 131072 | tf_op jit(solution)/shard_map/all_to_all | solution.py:21
  27.5 0.0 collective-permute-done
  27.5 0.0 collective-permute-done.1
  27.5 0.0 collective-permute-done.2
  27.6 0.0 copy-start.3
  27.6 2.0 %all_gather.3.refs_0_ = bf16[14,2,2,8,256]{4,3,2,1,0:T(8,128)(2,1)S(1)} all-gather(bf16[7,2,2,8,256]{4,3,2,1,0:T(8,128)(2,1)S(1)} %constant_dynamic-update-slice_fusion), channel_id=1, replica_groups={{0,1},{2,3},{4,5},{6,7},{8,9},{10,11},{12,13},{14,15},{16,17},{18,19},{..., dimensions={0}, use_global_device_ids=true | all-gather | bytes 344064 | tf_op jit(solution)/shard_map/all_gather | solution.py:41
  29.6 0.0 copy-start
  29.6 0.0 copy-start.1
  29.6 0.0 copy-start.2
  29.6 0.0 copy-done.3
  29.6 0.6 %copy-done = s32[2]{0:T(128)S(1)} copy-done((s32[2]{0:T(128)S(1)}, s32[2]{0:T(128)}, u32[]{:S(2)}) %copy-start) | copy-done | bytes 32
  30.2 0.0 copy-done.1
  30.2 0.0 copy-done.2
  30.2 0.8 %prepare.1 = (bf16[16,5632]{1,0:T(8,128)(2,1)S(1)}, bf16[16,5632]{1,0:T(8,128)(2,1)S(1)}, bf16[384,256]{1,0:T(8,128)(2,1)S(1)}, f32[16,512]{1,0:T(8,128)S(1)}, f...) custom-call(s32[1]{0:T(128)} %bitcast.1.place_ref, s32[2]{0:T(128)S(1)} %copy-done, s32[2]{0:T(128)S(1)} %copy-done.1, ...), custom_call_target="tpu_custom_call" | custom-call | flops 1048576 | bytes 1048576 | tf_op jit(solution)/shard_map/prepare/pallas_call | solution.py:204
  31.0 11.7 %all-to-all-done = f32[64,2,32]{2,1,0:T(2,128)S(1)} async-done(((f32[64,2,32]{2,1,0:T(2,128)}), f32[64,2,32]{2,1,0:T(2,128)S(1)}, u32[]{:S(2)}, u32[]{:S(2)}) %all-to-all-start) | async-done | bytes 16416 | tf_op jit(solution)/shard_map/all_to_all | solution.py:21
  42.7 1.7 %detect.1 = (bf16[2,2,8,512]{3,2,1,0:T(8,128)(2,1)S(1)}, f32[2,8,512]{2,1,0:T(8,128)}) custom-call(f32[128,32]{1,0:T(8,128)S(1)} %bitcast.16, bf16[16,5632]{1,0:T(8,128)(2,1)S(1)} %get-tuple-element.10.left_ref, bf16[16,5632]{1,0:T(8,128)(2,1)S(1)} %get-tuple-element.11.right_ref, bf16[384,256]{1,0:T(8,128)(2,1)S(1)} %get-tuple-element.12.window_ref, ...), custom_call_target="tpu_custom_call" | custom-call | flops 268435456 | bytes 1048576 | tf_op jit(solution)/shard_map/detect/pallas_call | solution.py:220
  44.4 0.6 %copy.11 = bf16[2,8,2,512]{3,2,1,0:T(2,128)(2,1)} copy(bf16[2,8,2,512]{3,1,2,0:T(8,128)(2,1)S(1)} %bitcast.17) | data formatting | bytes 65536
  (7 shorter events, 0.0 us)
Async XLA Ops:
  1.4 12.2 %copy-start.4 = (bf16[2,32]{1,0:T(2,128)(2,1)S(1)}, bf16[2,32]{1,0:T(2,128)(2,1)}, u32[]{:S(2)}) copy-start(bf16[2,32]{1,0:T(2,128)(2,1)} %param.7) | copy-start | bytes 388
  1.4 26.1 %collective-permute-start = (bf16[2,2,2,8,256]{4,3,2,1,0:T(8,128)(2,1)S(1)}, bf16[2,2,2,8,256]{4,3,2,1,0:T(8,128)(2,1)S(1)}, u32[]{:S(2)}, u32[]{:S(2)}) collective-permute-start(bf16[2,2,2,8,256]{4,3,2,1,0:T(8,128)(2,1)S(1)} %pad_maximum_fusion), channel_id=1, source_target_pairs={{2,0},{3,1},{4,2},{5,3},{6,4},{7,5},{10,8},{11,9},{12,10},{13,11},... | collective-permute-start | bytes 98312 | tf_op jit(solution)/shard_map/ppermute | solution.py:32
  4.1 23.4 %collective-permute-start.1 = (bf16[2,2,2,8,256]{4,3,2,1,0:T(8,128)(2,1)S(1)}, bf16[2,2,2,8,256]{4,3,2,1,0:T(8,128)(2,1)S(1)}, u32[]{:S(2)}, u32[]{:S(2)}) collective-permute-start(bf16[2,2,2,8,256]{4,3,2,1,0:T(8,128)(2,1)S(1)} %pad_maximum_fusion), channel_id=1, source_target_pairs={{4,0},{5,1},{6,2},{7,3},{12,8},{13,9},{14,10},{15,11},{20,16},{21,... | collective-permute-start | bytes 98312 | tf_op jit(solution)/shard_map/ppermute | solution.py:32
  12.3 15.3 %collective-permute-start.2 = (bf16[1,2,2,8,256]{4,3,2,1,0:T(8,128)(2,1)S(1)}, bf16[1,2,2,8,256]{4,3,2,1,0:T(8,128)(2,1)S(1)}, u32[]{:S(2)}, u32[]{:S(2)}) collective-permute-start(bf16[1,2,2,8,256]{4,3,2,1,0:T(8,128)(2,1)S(1)} %get-tuple-element.22), channel_id=1, source_target_pairs={{6,0},{1,3},{3,5},{5,7},{14,8},{9,11},{11,13},{13,15},{22,16},{17,... | collective-permute-start | bytes 49160 | tf_op jit(solution)/shard_map/ppermute | solution.py:32
  14.3 28.5 %all-to-all-start = ((f32[64,2,32]{2,1,0:T(2,128)}), f32[64,2,32]{2,1,0:T(2,128)S(1)}, u32[]{:S(2)}, u32[]{:S(2)}) async-start(f32[64,2,32]{2,1,0:T(2,128)} %broadcast_in_dim.3), calls=%async_computation | async-start | bytes 131072 | tf_op jit(solution)/shard_map/all_to_all | solution.py:21
  27.6 2.0 %copy-start.3 = (s32[2]{0:T(128)S(1)}, s32[2]{0:T(128)}, u32[]{:S(2)}) copy-start(s32[2]{0:T(128)} %offset_ref.1) | copy-start | bytes 28
  29.6 0.7 %copy-start = (s32[2]{0:T(128)S(1)}, s32[2]{0:T(128)}, u32[]{:S(2)}) copy-start(s32[2]{0:T(128)} %guard_ref.1) | copy-start | bytes 28
  29.6 0.7 %copy-start.1 = (s32[2]{0:T(128)S(1)}, s32[2]{0:T(128)}, u32[]{:S(2)}) copy-start(s32[2]{0:T(128)} %train_ref.1) | copy-start | bytes 28
  29.6 0.7 %copy-start.2 = (s32[2]{0:T(128)S(1)}, s32[2]{0:T(128)}, u32[]{:S(2)}) copy-start(s32[2]{0:T(128)} %scale_ref.1) | copy-start | bytes 28

commit v3 on v2

--- a/solution.py
+++ b/solution.py
@@ -41,17 +41,45 @@
     return lax.all_gather(mine, "range", axis_index_groups=chips, tiled=True)
 
 
-def prepare(shards, place_ref, guard_ref, train_ref, scale_ref, offset_ref, *refs):
-    strip_ref, outs = refs[0], refs[1:]
-    left_ref, right_ref, window_ref, slope_ref, floor_ref, edge_ref = outs
+def tables(shards, place_ref, guard_ref, train_ref, scale_ref, offset_ref, *outs):
+    window_ref, slope_ref, floor_ref, edge_ref, scalars_ref = outs
     place = place_ref[0]
+    scalars_ref[0] = offset_ref[0]
+    scalars_ref[1] = offset_ref[1]
+    scalars_ref[2] = lax.rem(place, 2)
+    apart = jnp.abs(
+        lax.broadcasted_iota(jnp.int32, (3 * TILE, TILE), 0)
+        - TILE
+        - lax.broadcasted_iota(jnp.int32, (3 * TILE, TILE), 1)
+    )
+    gate = place * (INNER * TILE) + lax.broadcasted_iota(jnp.int32, (8, INNER * TILE), 1)
+    last = shards * INNER * TILE - 1
+    for beam in range(2):
+        guard = guard_ref[beam]
+        train = train_ref[beam]
+        inside = jnp.logical_and(apart > guard, apart <= guard + train)
+        window_ref[:, beam * TILE : (beam + 1) * TILE] = jnp.where(inside, 1.0, 0.0).astype(
+            jnp.bfloat16
+        )
+        count = jnp.clip(gate - guard, 0, train) + jnp.clip(last - gate - guard, 0, train)
+        level = jnp.full((8, TILE), scale_ref[beam], jnp.int32).astype(jnp.float32)
+        factor = jnp.exp2(level / 8.0)
+        slope_ref[8 * beam : 8 * beam + 8, :] = jnp.concatenate(
+            [factor] * INNER, axis=1
+        ) / count.astype(jnp.float32)
+        floor_ref[8 * beam : 8 * beam + 8, :] = factor * EPSILON
+    edge_ref[0:8, :] = jnp.where(jnp.full((8, TILE), place, jnp.int32) > 0, 1.0, 0.0)
+    edge_ref[8:16, :] = jnp.where(jnp.full((8, TILE), place, jnp.int32) < shards - 1, 1.0, 0.0)
+
+
+def prepare(scalars_ref, strip_ref, left_ref, right_ref):
     lane = lax.broadcasted_iota(jnp.int32, (8, TILE), 1)
 
     count = strip_ref.shape[0] // 2
     strip = [2 * count - 1]
     strip += [core * count + at + sub for at in (0, 2, 4) for core in (0, 1) for sub in (0, 1)]
     strip += [count - 1]
-    core = lax.rem(place, 2)
+    core = scalars_ref[2]
     blocks = []
     for n in range(len(strip) - 2):
         piece = jnp.where(core == 0, strip[n], strip[n + 2])
@@ -59,7 +87,7 @@
 
     aligned = []
     for beam in range(2):
-        offset = offset_ref[beam]
+        offset = scalars_ref[beam]
         shift = lax.rem(TILE - offset, TILE)
         whole = lane < TILE - offset
         parts = []
@@ -80,30 +108,6 @@
         left_ref[:, at + TILE : at + 2 * TILE] = imag.astype(jnp.bfloat16)
         right_ref[:, at : at + TILE] = imag.astype(jnp.bfloat16)
         right_ref[:, at + TILE : at + 2 * TILE] = (-real).astype(jnp.bfloat16)
-
-    apart = jnp.abs(
-        lax.broadcasted_iota(jnp.int32, (3 * TILE, TILE), 0)
-        - TILE
-        - lax.broadcasted_iota(jnp.int32, (3 * TILE, TILE), 1)
-    )
-    gate = place * (INNER * TILE) + lax.broadcasted_iota(jnp.int32, (8, INNER * TILE), 1)
-    last = shards * INNER * TILE - 1
-    for beam in range(2):
-        guard = guard_ref[beam]
-        train = train_ref[beam]
-        inside = jnp.logical_and(apart > guard, apart <= guard + train)
-        window_ref[:, beam * TILE : (beam + 1) * TILE] = jnp.where(inside, 1.0, 0.0).astype(
-            jnp.bfloat16
-        )
-        count = jnp.clip(gate - guard, 0, train) + jnp.clip(last - gate - guard, 0, train)
-        level = jnp.full((8, TILE), scale_ref[beam], jnp.int32).astype(jnp.float32)
-        factor = jnp.exp2(level / 8.0)
-        slope_ref[8 * beam : 8 * beam + 8, :] = jnp.concatenate(
-            [factor] * INNER, axis=1
-        ) / count.astype(jnp.float32)
-        floor_ref[8 * beam : 8 * beam + 8, :] = factor * EPSILON
-    edge_ref[0:8, :] = jnp.where(jnp.full((8, TILE), place, jnp.int32) > 0, 1.0, 0.0)
-    edge_ref[8:16, :] = jnp.where(jnp.full((8, TILE), place, jnp.int32) < shards - 1, 1.0, 0.0)
 
 
 def detect(taps_ref, left_ref, right_ref, window_ref, slope_ref, floor_ref, edge_ref, *outs):
@@ -199,24 +203,31 @@
 
     taps = sent_to_all(replica.astype(f32), ("beam", "pulse"))
     strip = strip_of_chip(signal)
-    taps = taps.reshape(-1, taps.shape[-1])
-    place = lax.axis_index("range").reshape(1)
-    prepared = pl.pallas_call(
-        functools.partial(prepare, shards),
+    window, slope, floor, edge, scalars = pl.pallas_call(
+        functools.partial(tables, shards),
         out_shape=(
-            jax.ShapeDtypeStruct((16, 2 * BLOCKS * TILE), bf16),
-            jax.ShapeDtypeStruct((16, 2 * BLOCKS * TILE), bf16),
             jax.ShapeDtypeStruct((3 * TILE, 2 * TILE), bf16),
             jax.ShapeDtypeStruct((16, INNER * TILE), f32),
             jax.ShapeDtypeStruct((16, TILE), f32),
             jax.ShapeDtypeStruct((16, TILE), f32),
+            jax.ShapeDtypeStruct((3,), jnp.int32),
         ),
-        in_specs=[smem] * 5 + [vmem],
-        out_specs=[vmem] * 6,
+        in_specs=[smem] * 5,
+        out_specs=[vmem] * 4 + [smem],
+        compiler_params=pltpu.CompilerParams(vmem_limit_bytes=4 << 20),
+        cost_estimate=pl.CostEstimate(flops=1 << 20, bytes_accessed=1 << 18, transcendentals=0),
+        name="tables",
+    )(lax.axis_index("range").reshape(1), guard_cells, train_cells, scale_index, offsets)
+    taps = taps.reshape(-1, taps.shape[-1])
+    left, right = pl.pallas_call(
+        prepare,
+        out_shape=[jax.ShapeDtypeStruct((16, 2 * BLOCKS * TILE), bf16)] * 2,
+        in_specs=[smem, vmem],
+        out_specs=[vmem] * 2,
         compiler_params=pltpu.CompilerParams(vmem_limit_bytes=4 << 20),
         cost_estimate=pl.CostEstimate(flops=1 << 20, bytes_accessed=1 << 20, transcendentals=0),
         name="prepare",
-    )(place, guard_cells, train_cells, scale_index, offsets, strip)
+    )(scalars, strip)
     compressed, ratio = pl.pallas_call(
         detect,
         out_shape=(
@@ -228,7 +239,7 @@
         compiler_params=pltpu.CompilerParams(vmem_limit_bytes=4 << 20),
         cost_estimate=pl.CostEstimate(flops=1 << 28, bytes_accessed=1 << 20, transcendentals=0),
         name="detect",
-    )(taps, *prepared)
+    )(taps, left, right, window, slope, floor, edge)
     return jnp.transpose(compressed, (0, 2, 1, 3)), ratio
 
 

time: 45.3 us -> 45.3 us (level)
  waiting for transfers between devices: 11.7 us -> 10.6 us
  Pallas kernels: 2.42 us -> 3.5 us
    all_to_all x1, waiting for transfers between devices: 11.7 us -> 10.6 us  [sent_to_all(): return lax.all_to_all(copies, axis, split_axis=0, concat_axis=0, tiled=True)]
    pallas_call x1 -> x2, Pallas kernels: 0.76 us -> 1.83 us  [the longest x1 1.16 us: body(): pl.pallas_call(functools.partial(tables, shards), out_shape=(jax.ShapeDty...]
  transfers between devices with their start and end apart: 4 -> 4, of which waited for: 1 -> 1; matrix products, arithmetic and copies ran while one was open for 1% -> 1% of each run, Pallas kernels for 2% -> 4%
where the time goes in v3:
time: 45.3 us; the launch traced here: 45 us
  starting transfers between devices  25.3 us (56%)
  waiting for transfers between devices  10.6 us (23%)
  Pallas kernels  3.5 us (8%)
  local copies, waits for them, and re-layouts  2.74 us (6%)
  blocking collectives  1.97 us (4%)
  between operations  0.81 us (2%)
    all_to_all x1, starting transfers between devices, sent_to_all(): return lax.all_to_all(copies, axis, split_axis=0, concat_axis=0, tiled=True)  13.2 us
    ppermute x3, starting transfers between devices, sent(): return lax.ppermute(array, 'range', inside)  12.1 us
    all_to_all x1, waiting for transfers between devices, sent_to_all(): return lax.all_to_all(copies, axis, split_axis=0, concat_axis=0, tiled=True)  10.6 us
    unnamed x16, local copies, waits for them, and re-layouts  2.1 us
    all_gather x1, blocking collectives, strip_of_chip(): return lax.all_gather(mine, 'range', axis_index_groups=chips, tiled=True)  1.97 us
    pallas_call x1, Pallas kernels, body(): pl.pallas_call(detect, out_shape=(jax.ShapeDtypeStruct((2, 2, 8, INNER *...  1.67 us
    pallas_call x1, Pallas kernels, body(): pl.pallas_call(functools.partial(tables, shards), out_shape=(jax.ShapeDty...  1.16 us
  transfers between devices with their start and end apart: 4, of which 1 were waited for; matrix products, arithmetic and copies ran while one was open for 1% of the time, Pallas kernels for 4%

profile of v3, /device:TPU:24, one launch (start us, length us, event | category | flops | bytes accessed | tf_op | source)
XLA Modules:
  0.0 45.0 jit_solution(10541718043865658800)
XLA Ops:
  0.6 0.8 %copy.13 = bf16[2,8,2,512]{3,1,2,0:T(8,128)(2,1)S(1)} copy(bf16[2,8,2,512]{3,2,1,0:T(2,128)(2,1)} %param.6) | data formatting | bytes 65536 | tf_op args[0]
  1.4 0.0 copy-start.4
  1.4 2.6 %collective-permute-start = (bf16[2,2,2,8,256]{4,3,2,1,0:T(8,128)(2,1)S(1)}, bf16[2,2,2,8,256]{4,3,2,1,0:T(8,128)(2,1)S(1)}, u32[]{:S(2)}, u32[]{:S(2)}) collective-permute-start(bf16[2,2,2,8,256]{4,3,2,1,0:T(8,128)(2,1)S(1)} %pad_maximum_fusion), channel_id=1, source_target_pairs={{2,0},{3,1},{4,2},{5,3},{6,4},{7,5},{10,8},{11,9},{12,10},{13,11},... | collective-permute-start | bytes 98312 | tf_op jit(solution)/shard_map/ppermute | solution.py:32
  4.1 8.2 %collective-permute-start.1 = (bf16[2,2,2,8,256]{4,3,2,1,0:T(8,128)(2,1)S(1)}, bf16[2,2,2,8,256]{4,3,2,1,0:T(8,128)(2,1)S(1)}, u32[]{:S(2)}, u32[]{:S(2)}) collective-permute-start(bf16[2,2,2,8,256]{4,3,2,1,0:T(8,128)(2,1)S(1)} %pad_maximum_fusion), channel_id=1, source_target_pairs={{4,0},{5,1},{6,2},{7,3},{12,8},{13,9},{14,10},{15,11},{20,16},{21,... | collective-permute-start | bytes 98312 | tf_op jit(solution)/shard_map/ppermute | solution.py:32
  12.3 1.3 %collective-permute-start.2 = (bf16[1,2,2,8,256]{4,3,2,1,0:T(8,128)(2,1)S(1)}, bf16[1,2,2,8,256]{4,3,2,1,0:T(8,128)(2,1)S(1)}, u32[]{:S(2)}, u32[]{:S(2)}) collective-permute-start(bf16[1,2,2,8,256]{4,3,2,1,0:T(8,128)(2,1)S(1)} %get-tuple-element.24), channel_id=1, source_target_pairs={{6,0},{1,3},{3,5},{5,7},{14,8},{9,11},{11,13},{13,15},{22,16},{17,... | collective-permute-start | bytes 49160 | tf_op jit(solution)/shard_map/ppermute | solution.py:32
  13.6 0.6 %broadcast_in_dim.3 = f32[64,2,32]{2,1,0:T(2,128)} broadcast(bf16[2,32]{1,0:T(2,128)(2,1)S(1)} %copy-done.4), dimensions={1,2} | broadcast | bytes 16512 | tf_op jit(solution)/shard_map/broadcast_in_dim | solution.py:20
  14.2 13.2 %all-to-all-start = ((f32[64,2,32]{2,1,0:T(2,128)}), f32[64,2,32]{2,1,0:T(2,128)S(1)}, u32[]{:S(2)}, u32[]{:S(2)}) async-start(f32[64,2,32]{2,1,0:T(2,128)} %broadcast_in_dim.3), calls=%async_computation | async-start | bytes 131072 | tf_op jit(solution)/shard_map/all_to_all | solution.py:21
  27.5 0.0 copy-start.3
  27.5 0.0 copy-start
  27.5 0.0 copy-start.1
  27.5 0.0 copy-start.2
  27.5 0.6 %copy-done.3 = s32[2]{0:T(128)S(1)} copy-done((s32[2]{0:T(128)S(1)}, s32[2]{0:T(128)}, u32[]{:S(2)}) %copy-start.3) | copy-done | bytes 32
  28.1 0.0 copy-done
  28.2 0.0 copy-done.1
  28.2 0.0 copy-done.2
  28.2 1.2 %tables.1 = (bf16[384,256]{1,0:T(8,128)(2,1)S(1)}, f32[16,512]{1,0:T(8,128)S(1)}, f32[16,128]{1,0:T(8,128)S(1)}, f32[16,128]{1,0:T(8,128)S(1)}, s32[3]{0:T(128)S(1)}) custom-call(s32[1]{0:T(128)} %bitcast.1.place_ref, s32[2]{0:T(128)S(1)} %copy-done, s32[2]{0:T(128)S(1)} %copy-done.1, s32[2]{0:T(128)S(1)} %copy-done.2, s32[2]{0:T(128)S(1)} %copy-done.3), custom_call_target="tpu_custom_call" | custom-call | flops 1048576 | bytes 262144 | tf_op jit(solution)/shard_map/tables/pallas_call | solution.py:206
  29.4 0.0 collective-permute-done
  29.4 0.0 collective-permute-done.1
  29.4 0.0 collective-permute-done.2
  29.4 2.0 %all_gather.3.strip_ref = bf16[14,2,2,8,256]{4,3,2,1,0:T(8,128)(2,1)S(1)} all-gather(bf16[7,2,2,8,256]{4,3,2,1,0:T(8,128)(2,1)S(1)} %constant_dynamic-update-slice_fusion), channel_id=1, replica_groups={{0,1},{2,3},{4,5},{6,7},{8,9},{10,11},{12,13},{14,15},{16,17},{18,19},{..., dimensions={0}, use_global_device_ids=true | all-gather | bytes 344064 | tf_op jit(solution)/shard_map/all_gather | solution.py:41
  31.4 0.7 %prepare.1 = (bf16[16,5632]{1,0:T(8,128)(2,1)S(1)}, bf16[16,5632]{1,0:T(8,128)(2,1)S(1)}) custom-call(s32[3]{0:T(128)S(1)} %get-tuple-element.11.scalars_ref, bf16[14,2,2,8,256]{4,3,2,1,0:T(8,128)(2,1)S(1)} %all_gather.3.strip_ref), custom_call_target="tpu_custom_call" | custom-call | flops 1048576 | bytes 1048576 | tf_op jit(solution)/shard_map/prepare/pallas_call | solution.py:222
  32.1 10.6 %all-to-all-done = f32[64,2,32]{2,1,0:T(2,128)S(1)} async-done(((f32[64,2,32]{2,1,0:T(2,128)}), f32[64,2,32]{2,1,0:T(2,128)S(1)}, u32[]{:S(2)}, u32[]{:S(2)}) %all-to-all-start) | async-done | bytes 16416 | tf_op jit(solution)/shard_map/all_to_all | solution.py:21
  42.7 1.7 %detect.1 = (bf16[2,2,8,512]{3,2,1,0:T(8,128)(2,1)S(1)}, f32[2,8,512]{2,1,0:T(8,128)}) custom-call(f32[128,32]{1,0:T(8,128)S(1)} %bitcast.16, bf16[16,5632]{1,0:T(8,128)(2,1)S(1)} %get-tuple-element.12.left_ref, bf16[16,5632]{1,0:T(8,128)(2,1)S(1)} %get-tuple-element.13.right_ref, bf16[384,256]{1,0:T(8,128)(2,1)S(1)} %get-tuple-element.14.window_ref, ...), custom_call_target="tpu_custom_call" | custom-call | flops 268435456 | bytes 1048576 | tf_op jit(solution)/shard_map/detect/pallas_call | solution.py:231
  44.4 0.6 %copy.11 = bf16[2,8,2,512]{3,2,1,0:T(2,128)(2,1)} copy(bf16[2,8,2,512]{3,1,2,0:T(8,128)(2,1)S(1)} %bitcast.17) | data formatting | bytes 65536
  (8 shorter events, 0.0 us)
Async XLA Ops:
  1.4 12.2 %copy-start.4 = (bf16[2,32]{1,0:T(2,128)(2,1)S(1)}, bf16[2,32]{1,0:T(2,128)(2,1)}, u32[]{:S(2)}) copy-start(bf16[2,32]{1,0:T(2,128)(2,1)} %param.7) | copy-start | bytes 388
  1.4 27.9 %collective-permute-start = (bf16[2,2,2,8,256]{4,3,2,1,0:T(8,128)(2,1)S(1)}, bf16[2,2,2,8,256]{4,3,2,1,0:T(8,128)(2,1)S(1)}, u32[]{:S(2)}, u32[]{:S(2)}) collective-permute-start(bf16[2,2,2,8,256]{4,3,2,1,0:T(8,128)(2,1)S(1)} %pad_maximum_fusion), channel_id=1, source_target_pairs={{2,0},{3,1},{4,2},{5,3},{6,4},{7,5},{10,8},{11,9},{12,10},{13,11},... | collective-permute-start | bytes 98312 | tf_op jit(solution)/shard_map/ppermute | solution.py:32
  4.1 25.3 %collective-permute-start.1 = (bf16[2,2,2,8,256]{4,3,2,1,0:T(8,128)(2,1)S(1)}, bf16[2,2,2,8,256]{4,3,2,1,0:T(8,128)(2,1)S(1)}, u32[]{:S(2)}, u32[]{:S(2)}) collective-permute-start(bf16[2,2,2,8,256]{4,3,2,1,0:T(8,128)(2,1)S(1)} %pad_maximum_fusion), channel_id=1, source_target_pairs={{4,0},{5,1},{6,2},{7,3},{12,8},{13,9},{14,10},{15,11},{20,16},{21,... | collective-permute-start | bytes 98312 | tf_op jit(solution)/shard_map/ppermute | solution.py:32
  12.3 17.1 %collective-permute-start.2 = (bf16[1,2,2,8,256]{4,3,2,1,0:T(8,128)(2,1)S(1)}, bf16[1,2,2,8,256]{4,3,2,1,0:T(8,128)(2,1)S(1)}, u32[]{:S(2)}, u32[]{:S(2)}) collective-permute-start(bf16[1,2,2,8,256]{4,3,2,1,0:T(8,128)(2,1)S(1)} %get-tuple-element.24), channel_id=1, source_target_pairs={{6,0},{1,3},{3,5},{5,7},{14,8},{9,11},{11,13},{13,15},{22,16},{17,... | collective-permute-start | bytes 49160 | tf_op jit(solution)/shard_map/ppermute | solution.py:32
  14.2 28.5 %all-to-all-start = ((f32[64,2,32]{2,1,0:T(2,128)}), f32[64,2,32]{2,1,0:T(2,128)S(1)}, u32[]{:S(2)}, u32[]{:S(2)}) async-start(f32[64,2,32]{2,1,0:T(2,128)} %broadcast_in_dim.3), calls=%async_computation | async-start | bytes 131072 | tf_op jit(solution)/shard_map/all_to_all | solution.py:21
  27.5 0.7 %copy-start.3 = (s32[2]{0:T(128)S(1)}, s32[2]{0:T(128)}, u32[]{:S(2)}) copy-start(s32[2]{0:T(128)} %offset_ref.1) | copy-start | bytes 28
  27.5 0.7 %copy-start = (s32[2]{0:T(128)S(1)}, s32[2]{0:T(128)}, u32[]{:S(2)}) copy-start(s32[2]{0:T(128)} %guard_ref.1) | copy-start | bytes 28
  27.5 0.7 %copy-start.1 = (s32[2]{0:T(128)S(1)}, s32[2]{0:T(128)}, u32[]{:S(2)}) copy-start(s32[2]{0:T(128)} %train_ref.1) | copy-start | bytes 28
  27.5 0.7 %copy-start.2 = (s32[2]{0:T(128)S(1)}, s32[2]{0:T(128)}, u32[]{:S(2)}) copy-start(s32[2]{0:T(128)} %scale_ref.1) | copy-start | bytes 28

commit v4 on v3

--- a/solution.py
+++ b/solution.py
@@ -111,14 +111,15 @@
 
 
 def detect(taps_ref, left_ref, right_ref, window_ref, slope_ref, floor_ref, edge_ref, *outs):
-    compressed_ref, ratio_ref = outs
+    compressed_ref, ratio_ref, pairs_ref, lines_ref = outs
     across = (((1,), (1,)), ((), ()))
     lane = lax.broadcasted_iota(jnp.int32, (8, TILE), 1)
     row = lax.broadcasted_iota(jnp.int32, (8, TILE), 0)
 
+    lines_ref[...] = taps_ref[...].astype(jnp.float32)
     rows = []
     for part in range(2):
-        quarters = [taps_ref[pl.ds(2 * q + part, 16, stride=8), :] for q in range(4)]
+        quarters = [lines_ref[pl.ds(2 * q + part, 16, stride=8), :] for q in range(4)]
         rows.append(jnp.concatenate(quarters, axis=1))
 
     total = jnp.zeros((2 * TILES * 16, TILE), jnp.float32)
@@ -160,8 +161,12 @@
         if 1 <= tile <= INNER:
             at = (tile - 1) * TILE
             for beam in range(2):
-                compressed_ref[beam, 0, :, at : at + TILE] = real[8 * beam : 8 * beam + 8]
-                compressed_ref[beam, 1, :, at : at + TILE] = imag[8 * beam : 8 * beam + 8]
+                rows_of = slice(8 * beam, 8 * beam + 8)
+                spot = 2 * (tile - 1) + beam
+                pairs_ref[spot, pl.ds(0, 8, stride=2), :] = real.astype(jnp.float32)[rows_of]
+                pairs_ref[spot, pl.ds(1, 8, stride=2), :] = imag.astype(jnp.float32)[rows_of]
+                pairs = pairs_ref[spot].astype(jnp.bfloat16)
+                compressed_ref[beam, :, :, at : at + TILE] = pairs.reshape(8, 2, TILE)
         real = real.astype(jnp.float32)
         imag = imag.astype(jnp.float32)
         power.append(real * real + imag * imag)
@@ -201,7 +206,7 @@
     smem = pl.BlockSpec(memory_space=pltpu.SMEM)
     f32, bf16 = jnp.float32, jnp.bfloat16
 
-    taps = sent_to_all(replica.astype(f32), ("beam", "pulse"))
+    taps = sent_to_all(replica, ("beam", "pulse"))
     strip = strip_of_chip(signal)
     window, slope, floor, edge, scalars = pl.pallas_call(
         functools.partial(tables, shards),
@@ -231,16 +236,17 @@
     compressed, ratio = pl.pallas_call(
         detect,
         out_shape=(
-            jax.ShapeDtypeStruct((2, 2, 8, INNER * TILE), bf16),
+            jax.ShapeDtypeStruct((2, 8, 2, INNER * TILE), bf16),
             jax.ShapeDtypeStruct((2, 8, INNER * TILE), f32),
         ),
         in_specs=[vmem] * 7,
         out_specs=[vmem] * 2,
+        scratch_shapes=[pltpu.VMEM((2 * INNER, 16, TILE), f32), pltpu.VMEM(taps.shape, f32)],
         compiler_params=pltpu.CompilerParams(vmem_limit_bytes=4 << 20),
         cost_estimate=pl.CostEstimate(flops=1 << 28, bytes_accessed=1 << 20, transcendentals=0),
         name="detect",
     )(taps, left, right, window, slope, floor, edge)
-    return jnp.transpose(compressed, (0, 2, 1, 3)), ratio
+    return compressed, ratio
 
 
 def solution(mesh):

time: 45.3 us -> 44 us (0.971)
  local copies, waits for them, and re-layouts: 2.74 us -> 2.09 us
  waiting for transfers between devices: 10.6 us -> 9.97 us
    all_to_all x1, waiting for transfers between devices: 10.6 us -> 9.96 us  [sent_to_all(): return lax.all_to_all(copies, axis, split_axis=0, concat_axis=0, tiled=True)]
    unnamed x16 -> x15, local copies, waits for them, and re-layouts: 2.1 us -> 1.46 us
where the time goes in v4:
time: 44 us; the launch traced here: 43.7 us
  starting transfers between devices  25.3 us (58%)
  waiting for transfers between devices  9.97 us (23%)
  Pallas kernels  3.51 us (8%)
  local copies, waits for them, and re-layouts  2.09 us (5%)
  blocking collectives  1.97 us (4%)
  between operations  0.81 us (2%)
    all_to_all x1, starting transfers between devices, sent_to_all(): return lax.all_to_all(copies, axis, split_axis=0, concat_axis=0, tiled=True)  13.2 us
    ppermute x3, starting transfers between devices, sent(): return lax.ppermute(array, 'range', inside)  12.1 us
    all_to_all x1, waiting for transfers between devices, sent_to_all(): return lax.all_to_all(copies, axis, split_axis=0, concat_axis=0, tiled=True)  9.96 us
    all_gather x1, blocking collectives, strip_of_chip(): return lax.all_gather(mine, 'range', axis_index_groups=chips, tiled=True)  1.97 us
    pallas_call x1, Pallas kernels, body(): pl.pallas_call(detect, out_shape=(jax.ShapeDtypeStruct((2, 8, 2, INNER *...  1.68 us
    unnamed x15, local copies, waits for them, and re-layouts  1.46 us
    pallas_call x1, Pallas kernels, body(): pl.pallas_call(functools.partial(tables, shards), out_shape=(jax.ShapeDty...  1.16 us
  transfers between devices with their start and end apart: 4, of which 1 were waited for; matrix products, arithmetic and copies ran while one was open for 1% of the time, Pallas kernels for 4%

profile of v4, /device:TPU:24, one launch (start us, length us, event | category | flops | bytes accessed | tf_op | source)
XLA Modules:
  0.0 43.7 jit_solution(6180250648146304699)
XLA Ops:
  0.6 0.8 %copy.11 = bf16[2,8,2,512]{3,1,2,0:T(8,128)(2,1)S(1)} copy(bf16[2,8,2,512]{3,2,1,0:T(2,128)(2,1)} %param.6) | data formatting | bytes 65536 | tf_op args[0]
  1.4 0.0 copy-start.4
  1.4 2.6 %collective-permute-start = (bf16[2,2,2,8,256]{4,3,2,1,0:T(8,128)(2,1)S(1)}, bf16[2,2,2,8,256]{4,3,2,1,0:T(8,128)(2,1)S(1)}, u32[]{:S(2)}, u32[]{:S(2)}) collective-permute-start(bf16[2,2,2,8,256]{4,3,2,1,0:T(8,128)(2,1)S(1)} %pad_maximum_fusion), channel_id=1, source_target_pairs={{2,0},{3,1},{4,2},{5,3},{6,4},{7,5},{10,8},{11,9},{12,10},{13,11},... | collective-permute-start | bytes 98312 | tf_op jit(solution)/shard_map/ppermute | solution.py:32
  4.1 8.2 %collective-permute-start.1 = (bf16[2,2,2,8,256]{4,3,2,1,0:T(8,128)(2,1)S(1)}, bf16[2,2,2,8,256]{4,3,2,1,0:T(8,128)(2,1)S(1)}, u32[]{:S(2)}, u32[]{:S(2)}) collective-permute-start(bf16[2,2,2,8,256]{4,3,2,1,0:T(8,128)(2,1)S(1)} %pad_maximum_fusion), channel_id=1, source_target_pairs={{4,0},{5,1},{6,2},{7,3},{12,8},{13,9},{14,10},{15,11},{20,16},{21,... | collective-permute-start | bytes 98312 | tf_op jit(solution)/shard_map/ppermute | solution.py:32
  12.3 1.3 %collective-permute-start.2 = (bf16[1,2,2,8,256]{4,3,2,1,0:T(8,128)(2,1)S(1)}, bf16[1,2,2,8,256]{4,3,2,1,0:T(8,128)(2,1)S(1)}, u32[]{:S(2)}, u32[]{:S(2)}) collective-permute-start(bf16[1,2,2,8,256]{4,3,2,1,0:T(8,128)(2,1)S(1)} %get-tuple-element.16), channel_id=1, source_target_pairs={{6,0},{1,3},{3,5},{5,7},{14,8},{9,11},{11,13},{13,15},{22,16},{17,... | collective-permute-start | bytes 49160 | tf_op jit(solution)/shard_map/ppermute | solution.py:32
  13.6 0.0 copy-done.4
  13.6 0.6 %broadcast_in_dim.3 = bf16[64,2,32]{2,1,0:T(2,128)(2,1)} broadcast(bf16[2,32]{1,0:T(2,128)(2,1)S(1)} %copy-done.4), dimensions={1,2} | broadcast | bytes 8320 | tf_op jit(solution)/shard_map/broadcast_in_dim | solution.py:20
  14.2 13.2 %all-to-all-start = ((bf16[64,2,32]{2,1,0:T(2,128)(2,1)}), bf16[64,2,32]{2,1,0:T(2,128)(2,1)S(1)}, u32[]{:S(2)}, u32[]{:S(2)}) async-start(bf16[64,2,32]{2,1,0:T(2,128)(2,1)} %broadcast_in_dim.3), calls=%async_computation | async-start | bytes 65536 | tf_op jit(solution)/shard_map/all_to_all | solution.py:21
  27.5 0.0 copy-start.3
  27.5 0.0 copy-start
  27.5 0.0 copy-start.1
  27.5 0.0 copy-start.2
  27.5 0.6 %copy-done.3 = s32[2]{0:T(128)S(1)} copy-done((s32[2]{0:T(128)S(1)}, s32[2]{0:T(128)}, u32[]{:S(2)}) %copy-start.3) | copy-done | bytes 32
  28.1 0.0 copy-done
  28.2 0.0 copy-done.1
  28.2 0.0 copy-done.2
  28.2 1.2 %tables.1 = (bf16[384,256]{1,0:T(8,128)(2,1)S(1)}, f32[16,512]{1,0:T(8,128)S(1)}, f32[16,128]{1,0:T(8,128)S(1)}, f32[16,128]{1,0:T(8,128)S(1)}, s32[3]{0:T(128)S(1)}) custom-call(s32[1]{0:T(128)} %bitcast.1.place_ref, s32[2]{0:T(128)S(1)} %copy-done, s32[2]{0:T(128)S(1)} %copy-done.1, s32[2]{0:T(128)S(1)} %copy-done.2, s32[2]{0:T(128)S(1)} %copy-done.3), custom_call_target="tpu_custom_call" | custom-call | flops 1048576 | bytes 262144 | tf_op jit(solution)/shard_map/tables/pallas_call | solution.py:211
  29.4 0.0 collective-permute-done
  29.4 0.0 collective-permute-done.1
  29.4 0.0 collective-permute-done.2
  29.4 2.0 %all_gather.3.strip_ref = bf16[14,2,2,8,256]{4,3,2,1,0:T(8,128)(2,1)S(1)} all-gather(bf16[7,2,2,8,256]{4,3,2,1,0:T(8,128)(2,1)S(1)} %constant_dynamic-update-slice_fusion), channel_id=1, replica_groups={{0,1},{2,3},{4,5},{6,7},{8,9},{10,11},{12,13},{14,15},{16,17},{18,19},{..., dimensions={0}, use_global_device_ids=true | all-gather | bytes 344064 | tf_op jit(solution)/shard_map/all_gather | solution.py:41
  31.4 0.7 %prepare.1 = (bf16[16,5632]{1,0:T(8,128)(2,1)S(1)}, bf16[16,5632]{1,0:T(8,128)(2,1)S(1)}) custom-call(s32[3]{0:T(128)S(1)} %get-tuple-element.9.scalars_ref, bf16[14,2,2,8,256]{4,3,2,1,0:T(8,128)(2,1)S(1)} %all_gather.3.strip_ref), custom_call_target="tpu_custom_call" | custom-call | flops 1048576 | bytes 1048576 | tf_op jit(solution)/shard_map/prepare/pallas_call | solution.py:227
  32.1 10.0 %all-to-all-done = bf16[64,2,32]{2,1,0:T(2,128)(2,1)S(1)} async-done(((bf16[64,2,32]{2,1,0:T(2,128)(2,1)}), bf16[64,2,32]{2,1,0:T(2,128)(2,1)S(1)}, u32[]{:S(2)}, u32[]{:S(2)}) %all-to-all-start) | async-done | bytes 8224 | tf_op jit(solution)/shard_map/all_to_all | solution.py:21
  42.0 1.7 %detect.1 = (bf16[2,8,2,512]{3,2,1,0:T(2,128)(2,1)}, f32[2,8,512]{2,1,0:T(8,128)}) custom-call(bf16[128,32]{1,0:T(8,128)(2,1)S(1)} %bitcast.15, bf16[16,5632]{1,0:T(8,128)(2,1)S(1)} %get-tuple-element.10.left_ref, bf16[16,5632]{1,0:T(8,128)(2,1)S(1)} %get-tuple-element.11.right_ref, bf16[384,256]{1,0:T(8,128)(2,1)S(1)} %get-tuple-element.12.window_ref, ...), custom_call_target="tpu_custom_call" | custom-call | flops 268435456 | bytes 1048576 | tf_op jit(solution)/shard_map/detect/pallas_call | solution.py:236
  (7 shorter events, 0.0 us)
Async XLA Ops:
  1.4 12.2 %copy-start.4 = (bf16[2,32]{1,0:T(2,128)(2,1)S(1)}, bf16[2,32]{1,0:T(2,128)(2,1)}, u32[]{:S(2)}) copy-start(bf16[2,32]{1,0:T(2,128)(2,1)} %param.7) | copy-start | bytes 388
  1.4 27.9 %collective-permute-start = (bf16[2,2,2,8,256]{4,3,2,1,0:T(8,128)(2,1)S(1)}, bf16[2,2,2,8,256]{4,3,2,1,0:T(8,128)(2,1)S(1)}, u32[]{:S(2)}, u32[]{:S(2)}) collective-permute-start(bf16[2,2,2,8,256]{4,3,2,1,0:T(8,128)(2,1)S(1)} %pad_maximum_fusion), channel_id=1, source_target_pairs={{2,0},{3,1},{4,2},{5,3},{6,4},{7,5},{10,8},{11,9},{12,10},{13,11},... | collective-permute-start | bytes 98312 | tf_op jit(solution)/shard_map/ppermute | solution.py:32
  4.1 25.3 %collective-permute-start.1 = (bf16[2,2,2,8,256]{4,3,2,1,0:T(8,128)(2,1)S(1)}, bf16[2,2,2,8,256]{4,3,2,1,0:T(8,128)(2,1)S(1)}, u32[]{:S(2)}, u32[]{:S(2)}) collective-permute-start(bf16[2,2,2,8,256]{4,3,2,1,0:T(8,128)(2,1)S(1)} %pad_maximum_fusion), channel_id=1, source_target_pairs={{4,0},{5,1},{6,2},{7,3},{12,8},{13,9},{14,10},{15,11},{20,16},{21,... | collective-permute-start | bytes 98312 | tf_op jit(solution)/shard_map/ppermute | solution.py:32
  12.3 17.1 %collective-permute-start.2 = (bf16[1,2,2,8,256]{4,3,2,1,0:T(8,128)(2,1)S(1)}, bf16[1,2,2,8,256]{4,3,2,1,0:T(8,128)(2,1)S(1)}, u32[]{:S(2)}, u32[]{:S(2)}) collective-permute-start(bf16[1,2,2,8,256]{4,3,2,1,0:T(8,128)(2,1)S(1)} %get-tuple-element.16), channel_id=1, source_target_pairs={{6,0},{1,3},{3,5},{5,7},{14,8},{9,11},{11,13},{13,15},{22,16},{17,... | collective-permute-start | bytes 49160 | tf_op jit(solution)/shard_map/ppermute | solution.py:32
  14.2 27.8 %all-to-all-start = ((bf16[64,2,32]{2,1,0:T(2,128)(2,1)}), bf16[64,2,32]{2,1,0:T(2,128)(2,1)S(1)}, u32[]{:S(2)}, u32[]{:S(2)}) async-start(bf16[64,2,32]{2,1,0:T(2,128)(2,1)} %broadcast_in_dim.3), calls=%async_computation | async-start | bytes 65536 | tf_op jit(solution)/shard_map/all_to_all | solution.py:21
  27.5 0.7 %copy-start.3 = (s32[2]{0:T(128)S(1)}, s32[2]{0:T(128)}, u32[]{:S(2)}) copy-start(s32[2]{0:T(128)} %offset_ref.1) | copy-start | bytes 28
  27.5 0.7 %copy-start = (s32[2]{0:T(128)S(1)}, s32[2]{0:T(128)}, u32[]{:S(2)}) copy-start(s32[2]{0:T(128)} %guard_ref.1) | copy-start | bytes 28
  27.5 0.7 %copy-start.1 = (s32[2]{0:T(128)S(1)}, s32[2]{0:T(128)}, u32[]{:S(2)}) copy-start(s32[2]{0:T(128)} %train_ref.1) | copy-start | bytes 28
  27.5 0.7 %copy-start.2 = (s32[2]{0:T(128)S(1)}, s32[2]{0:T(128)}, u32[]{:S(2)}) copy-start(s32[2]{0:T(128)} %scale_ref.1) | copy-start | bytes 28

commit v5 on v4

--- a/solution.py
+++ b/solution.py
@@ -16,9 +16,16 @@
 BLOCKS = TILES + CHUNKS - 1
 
 
-def sent_to_all(array, axis):
-    copies = jnp.broadcast_to(array, (lax.axis_size(axis), *array.shape))
-    return lax.all_to_all(copies, axis, split_axis=0, concat_axis=0, tiled=True)
+FIRST = 12
+
+
+def sent_to_all(array, axes):
+    beams, pulses = (lax.axis_size(axis) for axis in axes)
+    order = [((FIRST + i) % beams) * pulses + j for i in range(beams) for j in range(pulses)]
+    copies = jnp.broadcast_to(array, (beams * pulses, *array.shape))
+    return lax.all_to_all(
+        copies, axes, split_axis=0, concat_axis=0, tiled=True, axis_index_groups=[order]
+    )
 
 
 def strip_of_chip(signal):
@@ -128,7 +135,8 @@
         rolled = []
         for part in range(2):
             if chunk < CHUNKS - 1:
-                line = jnp.broadcast_to(rows[part][chunk : chunk + 1, :], (8, TILE))
+                at = (chunk - FIRST) % (CHUNKS - 1)
+                line = jnp.broadcast_to(rows[part][at : at + 1, :], (8, TILE))
                 rolled.append(
                     [pltpu.roll(line, 8 * q, 1, stride=1, stride_axis=0) for q in range(16)]
                 )

time: 44 us -> 39.3 us (0.89)
  waiting for transfers between devices: 9.97 us -> 5.16 us
    all_to_all x1, waiting for transfers between devices: 9.96 us -> 5.15 us  [sent_to_all(): lax.all_to_all(copies, axes, split_axis=0, concat_axis=0, tiled=True, axi...]
  transfers between devices with their start and end apart: 4 -> 4, of which waited for: 1 -> 1; matrix products, arithmetic and copies ran while one was open for 1% -> 2% of each run, Pallas kernels for 4% -> 5%
where the time goes in v5:
time: 39.3 us; the launch traced here: 39 us
  starting transfers between devices  25.5 us (65%)
  waiting for transfers between devices  5.16 us (13%)
  Pallas kernels  3.52 us (9%)
  local copies, waits for them, and re-layouts  2.09 us (5%)
  blocking collectives  1.97 us (5%)
  between operations  0.81 us (2%)
    all_to_all x1, starting transfers between devices, sent_to_all(): lax.all_to_all(copies, axes, split_axis=0, concat_axis=0, tiled=True, axi...  13.3 us
    ppermute x3, starting transfers between devices, sent(): return lax.ppermute(array, 'range', inside)  12.1 us
    all_to_all x1, waiting for transfers between devices, sent_to_all(): lax.all_to_all(copies, axes, split_axis=0, concat_axis=0, tiled=True, axi...  5.15 us
    all_gather x1, blocking collectives, strip_of_chip(): return lax.all_gather(mine, 'range', axis_index_groups=chips, tiled=True)  1.97 us
    pallas_call x1, Pallas kernels, body(): pl.pallas_call(detect, out_shape=(jax.ShapeDtypeStruct((2, 8, 2, INNER *...  1.69 us
    unnamed x15, local copies, waits for them, and re-layouts  1.46 us
    pallas_call x1, Pallas kernels, body(): pl.pallas_call(functools.partial(tables, shards), out_shape=(jax.ShapeDty...  1.16 us
  transfers between devices with their start and end apart: 4, of which 1 were waited for; matrix products, arithmetic and copies ran while one was open for 2% of the time, Pallas kernels for 5%

profile of v5, /device:TPU:24, one launch (start us, length us, event | category | flops | bytes accessed | tf_op | source)
XLA Modules:
  0.0 39.0 jit_solution(2031062704969652211)
XLA Ops:
  0.6 0.8 %copy.11 = bf16[2,8,2,512]{3,1,2,0:T(8,128)(2,1)S(1)} copy(bf16[2,8,2,512]{3,2,1,0:T(2,128)(2,1)} %param.6) | data formatting | bytes 65536 | tf_op args[0]
  1.4 0.0 copy-start.4
  1.4 2.6 %collective-permute-start = (bf16[2,2,2,8,256]{4,3,2,1,0:T(8,128)(2,1)S(1)}, bf16[2,2,2,8,256]{4,3,2,1,0:T(8,128)(2,1)S(1)}, u32[]{:S(2)}, u32[]{:S(2)}) collective-permute-start(bf16[2,2,2,8,256]{4,3,2,1,0:T(8,128)(2,1)S(1)} %pad_maximum_fusion), channel_id=1, source_target_pairs={{2,0},{3,1},{4,2},{5,3},{6,4},{7,5},{10,8},{11,9},{12,10},{13,11},... | collective-permute-start | bytes 98312 | tf_op jit(solution)/shard_map/ppermute | solution.py:39
  4.1 8.2 %collective-permute-start.1 = (bf16[2,2,2,8,256]{4,3,2,1,0:T(8,128)(2,1)S(1)}, bf16[2,2,2,8,256]{4,3,2,1,0:T(8,128)(2,1)S(1)}, u32[]{:S(2)}, u32[]{:S(2)}) collective-permute-start(bf16[2,2,2,8,256]{4,3,2,1,0:T(8,128)(2,1)S(1)} %pad_maximum_fusion), channel_id=1, source_target_pairs={{4,0},{5,1},{6,2},{7,3},{12,8},{13,9},{14,10},{15,11},{20,16},{21,... | collective-permute-start | bytes 98312 | tf_op jit(solution)/shard_map/ppermute | solution.py:39
  12.3 1.3 %collective-permute-start.2 = (bf16[1,2,2,8,256]{4,3,2,1,0:T(8,128)(2,1)S(1)}, bf16[1,2,2,8,256]{4,3,2,1,0:T(8,128)(2,1)S(1)}, u32[]{:S(2)}, u32[]{:S(2)}) collective-permute-start(bf16[1,2,2,8,256]{4,3,2,1,0:T(8,128)(2,1)S(1)} %get-tuple-element.16), channel_id=1, source_target_pairs={{6,0},{1,3},{3,5},{5,7},{14,8},{9,11},{11,13},{13,15},{22,16},{17,... | collective-permute-start | bytes 49160 | tf_op jit(solution)/shard_map/ppermute | solution.py:39
  13.6 0.0 copy-done.4
  13.6 0.6 %broadcast_in_dim.3 = bf16[64,2,32]{2,1,0:T(2,128)(2,1)} broadcast(bf16[2,32]{1,0:T(2,128)(2,1)S(1)} %copy-done.4), dimensions={1,2} | broadcast | bytes 8320 | tf_op jit(solution)/shard_map/broadcast_in_dim | solution.py:25
  14.2 13.3 %all-to-all-start = ((bf16[64,2,32]{2,1,0:T(2,128)(2,1)}), bf16[64,2,32]{2,1,0:T(2,128)(2,1)S(1)}, u32[]{:S(2)}, u32[]{:S(2)}) async-start(bf16[64,2,32]{2,1,0:T(2,128)(2,1)} %broadcast_in_dim.3), calls=%async_computation | async-start | bytes 65536 | tf_op jit(solution)/shard_map/all_to_all | solution.py:26
  27.6 0.0 copy-start.3
  27.6 0.0 copy-start
  27.6 0.0 copy-start.1
  27.6 0.0 copy-start.2
  27.6 0.6 %copy-done.3 = s32[2]{0:T(128)S(1)} copy-done((s32[2]{0:T(128)S(1)}, s32[2]{0:T(128)}, u32[]{:S(2)}) %copy-start.3) | copy-done | bytes 32
  28.2 0.0 copy-done
  28.3 0.0 copy-done.1
  28.3 0.0 copy-done.2
  28.3 1.2 %tables.1 = (bf16[384,256]{1,0:T(8,128)(2,1)S(1)}, f32[16,512]{1,0:T(8,128)S(1)}, f32[16,128]{1,0:T(8,128)S(1)}, f32[16,128]{1,0:T(8,128)S(1)}, s32[3]{0:T(128)S(1)}) custom-call(s32[1]{0:T(128)} %bitcast.1.place_ref, s32[2]{0:T(128)S(1)} %copy-done, s32[2]{0:T(128)S(1)} %copy-done.1, s32[2]{0:T(128)S(1)} %copy-done.2, s32[2]{0:T(128)S(1)} %copy-done.3), custom_call_target="tpu_custom_call" | custom-call | flops 1048576 | bytes 262144 | tf_op jit(solution)/shard_map/tables/pallas_call | solution.py:219
  29.5 0.0 collective-permute-done
  29.5 0.0 collective-permute-done.1
  29.5 0.0 collective-permute-done.2
  29.5 2.0 %all_gather.3.strip_ref = bf16[14,2,2,8,256]{4,3,2,1,0:T(8,128)(2,1)S(1)} all-gather(bf16[7,2,2,8,256]{4,3,2,1,0:T(8,128)(2,1)S(1)} %constant_dynamic-update-slice_fusion), channel_id=1, replica_groups={{0,1},{2,3},{4,5},{6,7},{8,9},{10,11},{12,13},{14,15},{16,17},{18,19},{..., dimensions={0}, use_global_device_ids=true | all-gather | bytes 344064 | tf_op jit(solution)/shard_map/all_gather | solution.py:48
  31.5 0.7 %prepare.1 = (bf16[16,5632]{1,0:T(8,128)(2,1)S(1)}, bf16[16,5632]{1,0:T(8,128)(2,1)S(1)}) custom-call(s32[3]{0:T(128)S(1)} %get-tuple-element.9.scalars_ref, bf16[14,2,2,8,256]{4,3,2,1,0:T(8,128)(2,1)S(1)} %all_gather.3.strip_ref), custom_call_target="tpu_custom_call" | custom-call | flops 1048576 | bytes 1048576 | tf_op jit(solution)/shard_map/prepare/pallas_call | solution.py:235
  32.2 5.1 %all-to-all-done = bf16[64,2,32]{2,1,0:T(2,128)(2,1)S(1)} async-done(((bf16[64,2,32]{2,1,0:T(2,128)(2,1)}), bf16[64,2,32]{2,1,0:T(2,128)(2,1)S(1)}, u32[]{:S(2)}, u32[]{:S(2)}) %all-to-all-start) | async-done | bytes 8224 | tf_op jit(solution)/shard_map/all_to_all | solution.py:26
  37.3 1.7 %detect.1 = (bf16[2,8,2,512]{3,2,1,0:T(2,128)(2,1)}, f32[2,8,512]{2,1,0:T(8,128)}) custom-call(bf16[128,32]{1,0:T(8,128)(2,1)S(1)} %bitcast.15, bf16[16,5632]{1,0:T(8,128)(2,1)S(1)} %get-tuple-element.10.left_ref, bf16[16,5632]{1,0:T(8,128)(2,1)S(1)} %get-tuple-element.11.right_ref, bf16[384,256]{1,0:T(8,128)(2,1)S(1)} %get-tuple-element.12.window_ref, ...), custom_call_target="tpu_custom_call" | custom-call | flops 268435456 | bytes 1048576 | tf_op jit(solution)/shard_map/detect/pallas_call | solution.py:244
  (7 shorter events, 0.0 us)
Async XLA Ops:
  1.4 12.2 %copy-start.4 = (bf16[2,32]{1,0:T(2,128)(2,1)S(1)}, bf16[2,32]{1,0:T(2,128)(2,1)}, u32[]{:S(2)}) copy-start(bf16[2,32]{1,0:T(2,128)(2,1)} %param.7) | copy-start | bytes 388
  1.4 28.0 %collective-permute-start = (bf16[2,2,2,8,256]{4,3,2,1,0:T(8,128)(2,1)S(1)}, bf16[2,2,2,8,256]{4,3,2,1,0:T(8,128)(2,1)S(1)}, u32[]{:S(2)}, u32[]{:S(2)}) collective-permute-start(bf16[2,2,2,8,256]{4,3,2,1,0:T(8,128)(2,1)S(1)} %pad_maximum_fusion), channel_id=1, source_target_pairs={{2,0},{3,1},{4,2},{5,3},{6,4},{7,5},{10,8},{11,9},{12,10},{13,11},... | collective-permute-start | bytes 98312 | tf_op jit(solution)/shard_map/ppermute | solution.py:39
  4.1 25.4 %collective-permute-start.1 = (bf16[2,2,2,8,256]{4,3,2,1,0:T(8,128)(2,1)S(1)}, bf16[2,2,2,8,256]{4,3,2,1,0:T(8,128)(2,1)S(1)}, u32[]{:S(2)}, u32[]{:S(2)}) collective-permute-start(bf16[2,2,2,8,256]{4,3,2,1,0:T(8,128)(2,1)S(1)} %pad_maximum_fusion), channel_id=1, source_target_pairs={{4,0},{5,1},{6,2},{7,3},{12,8},{13,9},{14,10},{15,11},{20,16},{21,... | collective-permute-start | bytes 98312 | tf_op jit(solution)/shard_map/ppermute | solution.py:39
  12.3 17.2 %collective-permute-start.2 = (bf16[1,2,2,8,256]{4,3,2,1,0:T(8,128)(2,1)S(1)}, bf16[1,2,2,8,256]{4,3,2,1,0:T(8,128)(2,1)S(1)}, u32[]{:S(2)}, u32[]{:S(2)}) collective-permute-start(bf16[1,2,2,8,256]{4,3,2,1,0:T(8,128)(2,1)S(1)} %get-tuple-element.16), channel_id=1, source_target_pairs={{6,0},{1,3},{3,5},{5,7},{14,8},{9,11},{11,13},{13,15},{22,16},{17,... | collective-permute-start | bytes 49160 | tf_op jit(solution)/shard_map/ppermute | solution.py:39
  14.2 23.1 %all-to-all-start = ((bf16[64,2,32]{2,1,0:T(2,128)(2,1)}), bf16[64,2,32]{2,1,0:T(2,128)(2,1)S(1)}, u32[]{:S(2)}, u32[]{:S(2)}) async-start(bf16[64,2,32]{2,1,0:T(2,128)(2,1)} %broadcast_in_dim.3), calls=%async_computation | async-start | bytes 65536 | tf_op jit(solution)/shard_map/all_to_all | solution.py:26
  27.6 0.7 %copy-start.3 = (s32[2]{0:T(128)S(1)}, s32[2]{0:T(128)}, u32[]{:S(2)}) copy-start(s32[2]{0:T(128)} %offset_ref.1) | copy-start | bytes 28
  27.6 0.7 %copy-start = (s32[2]{0:T(128)S(1)}, s32[2]{0:T(128)}, u32[]{:S(2)}) copy-start(s32[2]{0:T(128)} %guard_ref.1) | copy-start | bytes 28
  27.6 0.7 %copy-start.1 = (s32[2]{0:T(128)S(1)}, s32[2]{0:T(128)}, u32[]{:S(2)}) copy-start(s32[2]{0:T(128)} %train_ref.1) | copy-start | bytes 28
  27.6 0.7 %copy-start.2 = (s32[2]{0:T(128)S(1)}, s32[2]{0:T(128)}, u32[]{:S(2)}) copy-start(s32[2]{0:T(128)} %scale_ref.1) | copy-start | bytes 28

commit v6 on v5

--- a/solution.py
+++ b/solution.py
@@ -16,6 +16,7 @@
 BLOCKS = TILES + CHUNKS - 1
 
 
+EARLY = 6
 FIRST = 12
 
 
@@ -34,15 +35,27 @@
     half = cells.shape[3] // 2
     own = jnp.stack([cells[..., :half], cells[..., half:]])
 
-    def sent(array, pairs):
-        inside = [(i, j) for i, j in pairs if 0 <= i < devices]
-        return lax.ppermute(array, "range", inside)
-
     first = lax.rem(lax.axis_index("range"), 2) == 0
     ends = [(j + 6 if j % 2 == 0 else j - 2, j) for j in range(devices)]
-    ahead = sent(own, [(j + 2, j) for j in range(devices)])
-    farther = sent(own, [(j + 4, j) for j in range(devices)])
-    rest = sent(jnp.where(first, own[:1], own[1:]), ends)
+    second = [(j + 4, j) for j in range(devices)]
+    near = [(j + 2, j) for j in range(devices)]
+    planes = lax.axis_size("beam")
+    early = lax.axis_index("beam") < EARLY
+
+    def sent(array, early_pairs, late_pairs):
+        pairs = [(b * devices + i, b * devices + j) for b in range(EARLY) for i, j in early_pairs]
+        pairs += [(b * devices + i, b * devices + j) for b in range(EARLY, planes) for i, j in late_pairs]
+        inside = [(i, j) for i, j in pairs if i // devices == j // devices and i >= 0]
+        return lax.ppermute(array, ("beam", "range"), inside)
+
+    edge = jnp.where(first, own[:1], own[1:])
+    got0 = sent(edge, ends, [])
+    got1 = sent(jnp.where(early, own, jnp.concatenate([edge, edge])), second, ends)
+    got2 = sent(own, near, second)
+    got3 = sent(own, [], near)
+    ahead = jnp.where(early, got2, got3)
+    farther = jnp.where(early, got1, got2)
+    rest = jnp.where(early, got0, got1[:1])
     mine = jnp.concatenate([own, ahead, farther, rest], axis=0)
     chips = [[2 * i, 2 * i + 1] for i in range(devices // 2)]
     return lax.all_gather(mine, "range", axis_index_groups=chips, tiled=True)
@@ -223,7 +236,7 @@
             jax.ShapeDtypeStruct((16, INNER * TILE), f32),
             jax.ShapeDtypeStruct((16, TILE), f32),
             jax.ShapeDtypeStruct((16, TILE), f32),
-            jax.ShapeDtypeStruct((3,), jnp.int32),
+            pltpu.SMEM((3,), jnp.int32),
         ),
         in_specs=[smem] * 5,
         out_specs=[vmem] * 4 + [smem],

time: 39.3 us -> 39.3 us (level)
  Pallas kernels: 3.52 us -> 2.49 us
  waiting for transfers between devices: 5.16 us -> 6.06 us
    all_to_all x1, waiting for transfers between devices: 5.15 us -> 6.05 us  [sent_to_all(): lax.all_to_all(copies, axes, split_axis=0, concat_axis=0, tiled=True, axi...]
    pallas_call x1, Pallas kernels: 0.67 us -> 0.13 us  [body(): pl.pallas_call(prepare, out_shape=[jax.ShapeDtypeStruct((16, 2 * BLOCKS *...]
    pallas_call x1, Pallas kernels: 1.16 us -> 0.68 us  [body(): pl.pallas_call(functools.partial(tables, shards), out_shape=(jax.ShapeDty...]
    ppermute x3 -> x4, starting transfers between devices: 12.1 us -> 12.2 us  [sent(): return lax.ppermute(array, ('beam', 'range'), inside)]
    unnamed x15 -> x13, local copies, waits for them, and re-layouts: 1.46 us -> 1.45 us
  transfers between devices with their start and end apart: 4 -> 5, of which waited for: 1 -> 1; matrix products, arithmetic and copies ran while one was open for 2% -> 2% of each run, Pallas kernels for 5% -> 2%
where the time goes in v6:
time: 39.3 us; the launch traced here: 39 us
  starting transfers between devices  25.5 us (65%)
  waiting for transfers between devices  6.06 us (15%)
  Pallas kernels  2.49 us (6%)
  local copies, waits for them, and re-layouts  2.08 us (5%)
  blocking collectives  1.97 us (5%)
  between operations  0.83 us (2%)
    all_to_all x1, starting transfers between devices, sent_to_all(): lax.all_to_all(copies, axes, split_axis=0, concat_axis=0, tiled=True, axi...  13.4 us
    ppermute x4, starting transfers between devices, sent(): return lax.ppermute(array, ('beam', 'range'), inside)  12.2 us
    all_to_all x1, waiting for transfers between devices, sent_to_all(): lax.all_to_all(copies, axes, split_axis=0, concat_axis=0, tiled=True, axi...  6.05 us
    all_gather x1, blocking collectives, strip_of_chip(): return lax.all_gather(mine, 'range', axis_index_groups=chips, tiled=True)  1.97 us
    pallas_call x1, Pallas kernels, body(): pl.pallas_call(detect, out_shape=(jax.ShapeDtypeStruct((2, 8, 2, INNER *...  1.69 us
    unnamed x13, local copies, waits for them, and re-layouts  1.45 us
  transfers between devices with their start and end apart: 5, of which 1 were waited for; matrix products, arithmetic and copies ran while one was open for 2% of the time, Pallas kernels for 2%

profile of v6, /device:TPU:24, one launch (start us, length us, event | category | flops | bytes accessed | tf_op | source)
XLA Modules:
  0.0 39.0 jit_solution(12966533692007991811)
XLA Ops:
  0.6 0.8 %copy.11 = bf16[2,8,2,512]{3,1,2,0:T(8,128)(2,1)S(1)} copy(bf16[2,8,2,512]{3,2,1,0:T(2,128)(2,1)} %param.6) | data formatting | bytes 65536 | tf_op args[0]
  1.4 0.0 copy-start.4
  1.4 2.6 %collective-permute-start = (bf16[2,2,2,8,256]{4,3,2,1,0:T(8,128)(2,1)S(1)}, bf16[2,2,2,8,256]{4,3,2,1,0:T(8,128)(2,1)S(1)}, u32[]{:S(2)}, u32[]{:S(2)}) collective-permute-start(bf16[2,2,2,8,256]{4,3,2,1,0:T(8,128)(2,1)S(1)} %get-tuple-element.17), channel_id=1, source_target_pairs={{2,0},{3,1},{4,2},{5,3},{6,4},{7,5},{34,32},{35,33},{36,34},{37,35... | collective-permute-start | bytes 98312 | tf_op jit(solution)/shard_map/ppermute | solution.py:49
  4.1 0.7 %collective-permute-start.1 = (bf16[2,2,2,8,256]{4,3,2,1,0:T(8,128)(2,1)S(1)}, bf16[2,2,2,8,256]{4,3,2,1,0:T(8,128)(2,1)S(1)}, u32[]{:S(2)}, u32[]{:S(2)}) collective-permute-start(bf16[2,2,2,8,256]{4,3,2,1,0:T(8,128)(2,1)S(1)} %get-tuple-element.17), channel_id=1, source_target_pairs={{194,192},{195,193},{196,194},{197,195},{198,196},{199,197},{226,2... | collective-permute-start | bytes 98312 | tf_op jit(solution)/shard_map/ppermute | solution.py:49
  4.8 6.1 %collective-permute-start.3 = (bf16[1,2,2,8,256]{4,3,2,1,0:T(8,128)(2,1)S(1)}, bf16[1,2,2,8,256]{4,3,2,1,0:T(8,128)(2,1)S(1)}, u32[]{:S(2)}, u32[]{:S(2)}) collective-permute-start(bf16[1,2,2,8,256]{4,3,2,1,0:T(8,128)(2,1)S(1)} %get-tuple-element.18), channel_id=1, source_target_pairs={{6,0},{1,3},{3,5},{5,7},{38,32},{33,35},{35,37},{37,39},{70,64},{6... | collective-permute-start | bytes 49160 | tf_op jit(solution)/shard_map/ppermute | solution.py:49
  10.9 2.7 %collective-permute-start.2 = (bf16[2,2,2,8,256]{4,3,2,1,0:T(8,128)(2,1)S(1)}, bf16[2,2,2,8,256]{4,3,2,1,0:T(8,128)(2,1)S(1)}, u32[]{:S(2)}, u32[]{:S(2)}) collective-permute-start(bf16[2,2,2,8,256]{4,3,2,1,0:T(8,128)(2,1)S(1)} %get-tuple-element.16), channel_id=1, source_target_pairs={{4,0},{5,1},{6,2},{7,3},{36,32},{37,33},{38,34},{39,35},{68,64},{6... | collective-permute-start | bytes 98312 | tf_op jit(solution)/shard_map/ppermute | solution.py:49
  13.7 0.6 %broadcast_in_dim.3 = bf16[64,2,32]{2,1,0:T(2,128)(2,1)} broadcast(bf16[2,32]{1,0:T(2,128)(2,1)S(1)} %copy-done.4), dimensions={1,2} | broadcast | bytes 8320 | tf_op jit(solution)/shard_map/broadcast_in_dim | solution.py:26
  14.3 13.4 %all-to-all-start = ((bf16[64,2,32]{2,1,0:T(2,128)(2,1)}), bf16[64,2,32]{2,1,0:T(2,128)(2,1)S(1)}, u32[]{:S(2)}, u32[]{:S(2)}) async-start(bf16[64,2,32]{2,1,0:T(2,128)(2,1)} %broadcast_in_dim.3), calls=%async_computation | async-start | bytes 65536 | tf_op jit(solution)/shard_map/all_to_all | solution.py:27
  27.7 0.0 copy-start.3
  27.7 0.0 copy-start
  27.7 0.0 copy-start.1
  27.7 0.0 copy-start.2
  27.7 0.6 %copy-done.3 = s32[2]{0:T(128)S(1)} copy-done((s32[2]{0:T(128)S(1)}, s32[2]{0:T(128)}, u32[]{:S(2)}) %copy-start.3) | copy-done | bytes 32
  28.3 0.0 copy-done
  28.3 0.0 copy-done.1
  28.4 0.0 copy-done.2
  28.4 0.7 %tables.1 = (bf16[384,256]{1,0:T(8,128)(2,1)S(1)}, f32[16,512]{1,0:T(8,128)S(1)}, f32[16,128]{1,0:T(8,128)S(1)}, f32[16,128]{1,0:T(8,128)S(1)}, s32[3]{0:T(128)S(4)}) custom-call(s32[1]{0:T(128)} %bitcast.1.place_ref, s32[2]{0:T(128)S(1)} %copy-done, s32[2]{0:T(128)S(1)} %copy-done.1, s32[2]{0:T(128)S(1)} %copy-done.2, s32[2]{0:T(128)S(1)} %copy-done.3), custom_call_target="tpu_custom_call" | custom-call | flops 1048576 | bytes 262144 | tf_op jit(solution)/shard_map/tables/pallas_call | solution.py:232
  29.1 0.0 collective-permute-done
  29.1 0.0 collective-permute-done.1
  29.1 0.0 collective-permute-done.2
  29.2 2.0 %all_gather.3.strip_ref = bf16[14,2,2,8,256]{4,3,2,1,0:T(8,128)(2,1)S(1)} all-gather(bf16[7,2,2,8,256]{4,3,2,1,0:T(8,128)(2,1)S(1)} %fusion), channel_id=1, replica_groups={{0,1},{2,3},{4,5},{6,7},{8,9},{10,11},{12,13},{14,15},{16,17},{18,19},{..., dimensions={0}, use_global_device_ids=true | all-gather | bytes 344064 | tf_op jit(solution)/shard_map/all_gather | solution.py:61
  31.1 0.1 prepare.1
  31.3 6.0 %all-to-all-done = bf16[64,2,32]{2,1,0:T(2,128)(2,1)S(1)} async-done(((bf16[64,2,32]{2,1,0:T(2,128)(2,1)}), bf16[64,2,32]{2,1,0:T(2,128)(2,1)S(1)}, u32[]{:S(2)}, u32[]{:S(2)}) %all-to-all-start) | async-done | bytes 8224 | tf_op jit(solution)/shard_map/all_to_all | solution.py:27
  37.3 1.7 %detect.1 = (bf16[2,8,2,512]{3,2,1,0:T(2,128)(2,1)}, f32[2,8,512]{2,1,0:T(8,128)}) custom-call(bf16[128,32]{1,0:T(8,128)(2,1)S(1)} %bitcast.15, bf16[16,5632]{1,0:T(8,128)(2,1)S(1)} %get-tuple-element.10.left_ref, bf16[16,5632]{1,0:T(8,128)(2,1)S(1)} %get-tuple-element.11.right_ref, bf16[384,256]{1,0:T(8,128)(2,1)S(1)} %get-tuple-element.12.window_ref, ...), custom_call_target="tpu_custom_call" | custom-call | flops 268435456 | bytes 1048576 | tf_op jit(solution)/shard_map/detect/pallas_call | solution.py:257
  (9 shorter events, 0.1 us)
Async XLA Ops:
  1.4 12.2 %copy-start.4 = (bf16[2,32]{1,0:T(2,128)(2,1)S(1)}, bf16[2,32]{1,0:T(2,128)(2,1)}, u32[]{:S(2)}) copy-start(bf16[2,32]{1,0:T(2,128)(2,1)} %param.7) | copy-start | bytes 388
  1.4 27.6 %collective-permute-start = (bf16[2,2,2,8,256]{4,3,2,1,0:T(8,128)(2,1)S(1)}, bf16[2,2,2,8,256]{4,3,2,1,0:T(8,128)(2,1)S(1)}, u32[]{:S(2)}, u32[]{:S(2)}) collective-permute-start(bf16[2,2,2,8,256]{4,3,2,1,0:T(8,128)(2,1)S(1)} %get-tuple-element.17), channel_id=1, source_target_pairs={{2,0},{3,1},{4,2},{5,3},{6,4},{7,5},{34,32},{35,33},{36,34},{37,35... | collective-permute-start | bytes 98312 | tf_op jit(solution)/shard_map/ppermute | solution.py:49
  4.1 25.0 %collective-permute-start.1 = (bf16[2,2,2,8,256]{4,3,2,1,0:T(8,128)(2,1)S(1)}, bf16[2,2,2,8,256]{4,3,2,1,0:T(8,128)(2,1)S(1)}, u32[]{:S(2)}, u32[]{:S(2)}) collective-permute-start(bf16[2,2,2,8,256]{4,3,2,1,0:T(8,128)(2,1)S(1)} %get-tuple-element.17), channel_id=1, source_target_pairs={{194,192},{195,193},{196,194},{197,195},{198,196},{199,197},{226,2... | collective-permute-start | bytes 98312 | tf_op jit(solution)/shard_map/ppermute | solution.py:49
  4.8 24.4 %collective-permute-start.3 = (bf16[1,2,2,8,256]{4,3,2,1,0:T(8,128)(2,1)S(1)}, bf16[1,2,2,8,256]{4,3,2,1,0:T(8,128)(2,1)S(1)}, u32[]{:S(2)}, u32[]{:S(2)}) collective-permute-start(bf16[1,2,2,8,256]{4,3,2,1,0:T(8,128)(2,1)S(1)} %get-tuple-element.18), channel_id=1, source_target_pairs={{6,0},{1,3},{3,5},{5,7},{38,32},{33,35},{35,37},{37,39},{70,64},{6... | collective-permute-start | bytes 49160 | tf_op jit(solution)/shard_map/ppermute | solution.py:49
  10.9 18.2 %collective-permute-start.2 = (bf16[2,2,2,8,256]{4,3,2,1,0:T(8,128)(2,1)S(1)}, bf16[2,2,2,8,256]{4,3,2,1,0:T(8,128)(2,1)S(1)}, u32[]{:S(2)}, u32[]{:S(2)}) collective-permute-start(bf16[2,2,2,8,256]{4,3,2,1,0:T(8,128)(2,1)S(1)} %get-tuple-element.16), channel_id=1, source_target_pairs={{4,0},{5,1},{6,2},{7,3},{36,32},{37,33},{38,34},{39,35},{68,64},{6... | collective-permute-start | bytes 98312 | tf_op jit(solution)/shard_map/ppermute | solution.py:49
  14.3 23.0 %all-to-all-start = ((bf16[64,2,32]{2,1,0:T(2,128)(2,1)}), bf16[64,2,32]{2,1,0:T(2,128)(2,1)S(1)}, u32[]{:S(2)}, u32[]{:S(2)}) async-start(bf16[64,2,32]{2,1,0:T(2,128)(2,1)} %broadcast_in_dim.3), calls=%async_computation | async-start | bytes 65536 | tf_op jit(solution)/shard_map/all_to_all | solution.py:27
  27.7 0.7 %copy-start.3 = (s32[2]{0:T(128)S(1)}, s32[2]{0:T(128)}, u32[]{:S(2)}) copy-start(s32[2]{0:T(128)} %offset_ref.1) | copy-start | bytes 28
  27.7 0.7 %copy-start = (s32[2]{0:T(128)S(1)}, s32[2]{0:T(128)}, u32[]{:S(2)}) copy-start(s32[2]{0:T(128)} %guard_ref.1) | copy-start | bytes 28
  27.7 0.7 %copy-start.1 = (s32[2]{0:T(128)S(1)}, s32[2]{0:T(128)}, u32[]{:S(2)}) copy-start(s32[2]{0:T(128)} %train_ref.1) | copy-start | bytes 28
  27.7 0.7 %copy-start.2 = (s32[2]{0:T(128)S(1)}, s32[2]{0:T(128)}, u32[]{:S(2)}) copy-start(s32[2]{0:T(128)} %scale_ref.1) | copy-start | bytes 28

commit v7 on v6

--- a/solution.py
+++ b/solution.py
@@ -16,7 +16,7 @@
 BLOCKS = TILES + CHUNKS - 1
 
 
-EARLY = 6
+EARLY = 5
 FIRST = 12
 
 
@@ -49,13 +49,13 @@
         return lax.ppermute(array, ("beam", "range"), inside)
 
     edge = jnp.where(first, own[:1], own[1:])
-    got0 = sent(edge, ends, [])
-    got1 = sent(jnp.where(early, own, jnp.concatenate([edge, edge])), second, ends)
+    got0 = sent(own, second, [])
+    got1 = sent(edge, ends, ends)
     got2 = sent(own, near, second)
     got3 = sent(own, [], near)
     ahead = jnp.where(early, got2, got3)
-    farther = jnp.where(early, got1, got2)
-    rest = jnp.where(early, got0, got1[:1])
+    farther = jnp.where(early, got0, got2)
+    rest = got1
     mine = jnp.concatenate([own, ahead, farther, rest], axis=0)
     chips = [[2 * i, 2 * i + 1] for i in range(devices // 2)]
     return lax.all_gather(mine, "range", axis_index_groups=chips, tiled=True)

time: 39.3 us -> 39.4 us (level)
    all_to_all x1, starting transfers between devices: 13.4 us -> 12.7 us  [sent_to_all(): lax.all_to_all(copies, axes, split_axis=0, concat_axis=0, tiled=True, axi...]
    ppermute x4, starting transfers between devices: 12.2 us -> 12.8 us  [sent(): return lax.ppermute(array, ('beam', 'range'), inside)]
where the time goes in v7:
time: 39.4 us; the launch traced here: 39.1 us
  starting transfers between devices  25.5 us (65%)
  waiting for transfers between devices  6.15 us (16%)
  Pallas kernels  2.49 us (6%)
  local copies, waits for them, and re-layouts  2.08 us (5%)
  blocking collectives  1.97 us (5%)
  between operations  0.83 us (2%)
    ppermute x4, starting transfers between devices, sent(): return lax.ppermute(array, ('beam', 'range'), inside)  12.8 us
    all_to_all x1, starting transfers between devices, sent_to_all(): lax.all_to_all(copies, axes, split_axis=0, concat_axis=0, tiled=True, axi...  12.7 us
    all_to_all x1, waiting for transfers between devices, sent_to_all(): lax.all_to_all(copies, axes, split_axis=0, concat_axis=0, tiled=True, axi...  6.14 us
    all_gather x1, blocking collectives, strip_of_chip(): return lax.all_gather(mine, 'range', axis_index_groups=chips, tiled=True)  1.97 us
    pallas_call x1, Pallas kernels, body(): pl.pallas_call(detect, out_shape=(jax.ShapeDtypeStruct((2, 8, 2, INNER *...  1.69 us
    unnamed x13, local copies, waits for them, and re-layouts  1.45 us
  transfers between devices with their start and end apart: 5, of which 1 were waited for; matrix products, arithmetic and copies ran while one was open for 2% of the time, Pallas kernels for 2%

profile of v7, /device:TPU:24, one launch (start us, length us, event | category | flops | bytes accessed | tf_op | source)
XLA Modules:
  0.0 39.1 jit_solution(17907250774513544845)
XLA Ops:
  0.6 0.8 %copy.11 = bf16[2,8,2,512]{3,1,2,0:T(8,128)(2,1)S(1)} copy(bf16[2,8,2,512]{3,2,1,0:T(2,128)(2,1)} %param.6) | data formatting | bytes 65536 | tf_op args[0]
  1.4 0.0 copy-start.4
  1.4 2.6 %collective-permute-start = (bf16[2,2,2,8,256]{4,3,2,1,0:T(8,128)(2,1)S(1)}, bf16[2,2,2,8,256]{4,3,2,1,0:T(8,128)(2,1)S(1)}, u32[]{:S(2)}, u32[]{:S(2)}) collective-permute-start(bf16[2,2,2,8,256]{4,3,2,1,0:T(8,128)(2,1)S(1)} %pad_maximum_fusion), channel_id=1, source_target_pairs={{2,0},{3,1},{4,2},{5,3},{6,4},{7,5},{34,32},{35,33},{36,34},{37,35... | collective-permute-start | bytes 98312 | tf_op jit(solution)/shard_map/ppermute | solution.py:49
  4.1 0.7 %collective-permute-start.1 = (bf16[2,2,2,8,256]{4,3,2,1,0:T(8,128)(2,1)S(1)}, bf16[2,2,2,8,256]{4,3,2,1,0:T(8,128)(2,1)S(1)}, u32[]{:S(2)}, u32[]{:S(2)}) collective-permute-start(bf16[2,2,2,8,256]{4,3,2,1,0:T(8,128)(2,1)S(1)} %pad_maximum_fusion), channel_id=1, source_target_pairs={{162,160},{163,161},{164,162},{165,163},{166,164},{167,165},{194,1... | collective-permute-start | bytes 98312 | tf_op jit(solution)/shard_map/ppermute | solution.py:49
  4.8 8.2 %collective-permute-start.2 = (bf16[2,2,2,8,256]{4,3,2,1,0:T(8,128)(2,1)S(1)}, bf16[2,2,2,8,256]{4,3,2,1,0:T(8,128)(2,1)S(1)}, u32[]{:S(2)}, u32[]{:S(2)}) collective-permute-start(bf16[2,2,2,8,256]{4,3,2,1,0:T(8,128)(2,1)S(1)} %pad_maximum_fusion), channel_id=1, source_target_pairs={{4,0},{5,1},{6,2},{7,3},{36,32},{37,33},{38,34},{39,35},{68,64},{6... | collective-permute-start | bytes 98312 | tf_op jit(solution)/shard_map/ppermute | solution.py:49
  13.0 1.3 %collective-permute-start.3 = (bf16[1,2,2,8,256]{4,3,2,1,0:T(8,128)(2,1)S(1)}, bf16[1,2,2,8,256]{4,3,2,1,0:T(8,128)(2,1)S(1)}, u32[]{:S(2)}, u32[]{:S(2)}) collective-permute-start(bf16[1,2,2,8,256]{4,3,2,1,0:T(8,128)(2,1)S(1)} %get-tuple-element.16), channel_id=1, source_target_pairs={{6,0},{1,3},{3,5},{5,7},{38,32},{33,35},{35,37},{37,39},{70,64},{6... | collective-permute-start | bytes 49160 | tf_op jit(solution)/shard_map/ppermute | solution.py:49
  14.3 0.6 %broadcast_in_dim.3 = bf16[64,2,32]{2,1,0:T(2,128)(2,1)} broadcast(bf16[2,32]{1,0:T(2,128)(2,1)S(1)} %copy-done.4), dimensions={1,2} | broadcast | bytes 8320 | tf_op jit(solution)/shard_map/broadcast_in_dim | solution.py:26
  14.9 12.7 %all-to-all-start = ((bf16[64,2,32]{2,1,0:T(2,128)(2,1)}), bf16[64,2,32]{2,1,0:T(2,128)(2,1)S(1)}, u32[]{:S(2)}, u32[]{:S(2)}) async-start(bf16[64,2,32]{2,1,0:T(2,128)(2,1)} %broadcast_in_dim.3), calls=%async_computation | async-start | bytes 65536 | tf_op jit(solution)/shard_map/all_to_all | solution.py:27
  27.7 0.0 copy-start.3
  27.7 0.0 copy-start
  27.7 0.0 copy-start.1
  27.7 0.0 copy-start.2
  27.7 0.6 %copy-done.3 = s32[2]{0:T(128)S(1)} copy-done((s32[2]{0:T(128)S(1)}, s32[2]{0:T(128)}, u32[]{:S(2)}) %copy-start.3) | copy-done | bytes 32
  28.3 0.0 copy-done
  28.3 0.0 copy-done.1
  28.4 0.0 copy-done.2
  28.4 0.7 %tables.1 = (bf16[384,256]{1,0:T(8,128)(2,1)S(1)}, f32[16,512]{1,0:T(8,128)S(1)}, f32[16,128]{1,0:T(8,128)S(1)}, f32[16,128]{1,0:T(8,128)S(1)}, s32[3]{0:T(128)S(4)}) custom-call(s32[1]{0:T(128)} %bitcast.1.place_ref, s32[2]{0:T(128)S(1)} %copy-done, s32[2]{0:T(128)S(1)} %copy-done.1, s32[2]{0:T(128)S(1)} %copy-done.2, s32[2]{0:T(128)S(1)} %copy-done.3), custom_call_target="tpu_custom_call" | custom-call | flops 1048576 | bytes 262144 | tf_op jit(solution)/shard_map/tables/pallas_call | solution.py:232
  29.1 0.0 collective-permute-done.1
  29.1 0.0 collective-permute-done.2
  29.1 0.0 collective-permute-done.3
  29.2 2.0 %all_gather.3.strip_ref = bf16[14,2,2,8,256]{4,3,2,1,0:T(8,128)(2,1)S(1)} all-gather(bf16[7,2,2,8,256]{4,3,2,1,0:T(8,128)(2,1)S(1)} %constant_dynamic-update-slice_fusion), channel_id=1, replica_groups={{0,1},{2,3},{4,5},{6,7},{8,9},{10,11},{12,13},{14,15},{16,17},{18,19},{..., dimensions={0}, use_global_device_ids=true | all-gather | bytes 344064 | tf_op jit(solution)/shard_map/all_gather | solution.py:61
  31.1 0.1 prepare.1
  31.3 6.1 %all-to-all-done = bf16[64,2,32]{2,1,0:T(2,128)(2,1)S(1)} async-done(((bf16[64,2,32]{2,1,0:T(2,128)(2,1)}), bf16[64,2,32]{2,1,0:T(2,128)(2,1)S(1)}, u32[]{:S(2)}, u32[]{:S(2)}) %all-to-all-start) | async-done | bytes 8224 | tf_op jit(solution)/shard_map/all_to_all | solution.py:27
  37.4 1.7 %detect.1 = (bf16[2,8,2,512]{3,2,1,0:T(2,128)(2,1)}, f32[2,8,512]{2,1,0:T(8,128)}) custom-call(bf16[128,32]{1,0:T(8,128)(2,1)S(1)} %bitcast.15, bf16[16,5632]{1,0:T(8,128)(2,1)S(1)} %get-tuple-element.10.left_ref, bf16[16,5632]{1,0:T(8,128)(2,1)S(1)} %get-tuple-element.11.right_ref, bf16[384,256]{1,0:T(8,128)(2,1)S(1)} %get-tuple-element.12.window_ref, ...), custom_call_target="tpu_custom_call" | custom-call | flops 268435456 | bytes 1048576 | tf_op jit(solution)/shard_map/detect/pallas_call | solution.py:257
  (9 shorter events, 0.1 us)
Async XLA Ops:
  1.4 12.8 %copy-start.4 = (bf16[2,32]{1,0:T(2,128)(2,1)S(1)}, bf16[2,32]{1,0:T(2,128)(2,1)}, u32[]{:S(2)}) copy-start(bf16[2,32]{1,0:T(2,128)(2,1)} %param.7) | copy-start | bytes 388
  1.4 27.6 %collective-permute-start = (bf16[2,2,2,8,256]{4,3,2,1,0:T(8,128)(2,1)S(1)}, bf16[2,2,2,8,256]{4,3,2,1,0:T(8,128)(2,1)S(1)}, u32[]{:S(2)}, u32[]{:S(2)}) collective-permute-start(bf16[2,2,2,8,256]{4,3,2,1,0:T(8,128)(2,1)S(1)} %pad_maximum_fusion), channel_id=1, source_target_pairs={{2,0},{3,1},{4,2},{5,3},{6,4},{7,5},{34,32},{35,33},{36,34},{37,35... | collective-permute-start | bytes 98312 | tf_op jit(solution)/shard_map/ppermute | solution.py:49
  4.1 25.0 %collective-permute-start.1 = (bf16[2,2,2,8,256]{4,3,2,1,0:T(8,128)(2,1)S(1)}, bf16[2,2,2,8,256]{4,3,2,1,0:T(8,128)(2,1)S(1)}, u32[]{:S(2)}, u32[]{:S(2)}) collective-permute-start(bf16[2,2,2,8,256]{4,3,2,1,0:T(8,128)(2,1)S(1)} %pad_maximum_fusion), channel_id=1, source_target_pairs={{162,160},{163,161},{164,162},{165,163},{166,164},{167,165},{194,1... | collective-permute-start | bytes 98312 | tf_op jit(solution)/shard_map/ppermute | solution.py:49
  4.8 24.3 %collective-permute-start.2 = (bf16[2,2,2,8,256]{4,3,2,1,0:T(8,128)(2,1)S(1)}, bf16[2,2,2,8,256]{4,3,2,1,0:T(8,128)(2,1)S(1)}, u32[]{:S(2)}, u32[]{:S(2)}) collective-permute-start(bf16[2,2,2,8,256]{4,3,2,1,0:T(8,128)(2,1)S(1)} %pad_maximum_fusion), channel_id=1, source_target_pairs={{4,0},{5,1},{6,2},{7,3},{36,32},{37,33},{38,34},{39,35},{68,64},{6... | collective-permute-start | bytes 98312 | tf_op jit(solution)/shard_map/ppermute | solution.py:49
  13.0 16.2 %collective-permute-start.3 = (bf16[1,2,2,8,256]{4,3,2,1,0:T(8,128)(2,1)S(1)}, bf16[1,2,2,8,256]{4,3,2,1,0:T(8,128)(2,1)S(1)}, u32[]{:S(2)}, u32[]{:S(2)}) collective-permute-start(bf16[1,2,2,8,256]{4,3,2,1,0:T(8,128)(2,1)S(1)} %get-tuple-element.16), channel_id=1, source_target_pairs={{6,0},{1,3},{3,5},{5,7},{38,32},{33,35},{35,37},{37,39},{70,64},{6... | collective-permute-start | bytes 49160 | tf_op jit(solution)/shard_map/ppermute | solution.py:49
  14.9 22.5 %all-to-all-start = ((bf16[64,2,32]{2,1,0:T(2,128)(2,1)}), bf16[64,2,32]{2,1,0:T(2,128)(2,1)S(1)}, u32[]{:S(2)}, u32[]{:S(2)}) async-start(bf16[64,2,32]{2,1,0:T(2,128)(2,1)} %broadcast_in_dim.3), calls=%async_computation | async-start | bytes 65536 | tf_op jit(solution)/shard_map/all_to_all | solution.py:27
  27.7 0.7 %copy-start.3 = (s32[2]{0:T(128)S(1)}, s32[2]{0:T(128)}, u32[]{:S(2)}) copy-start(s32[2]{0:T(128)} %offset_ref.1) | copy-start | bytes 28
  27.7 0.7 %copy-start = (s32[2]{0:T(128)S(1)}, s32[2]{0:T(128)}, u32[]{:S(2)}) copy-start(s32[2]{0:T(128)} %guard_ref.1) | copy-start | bytes 28
  27.7 0.7 %copy-start.1 = (s32[2]{0:T(128)S(1)}, s32[2]{0:T(128)}, u32[]{:S(2)}) copy-start(s32[2]{0:T(128)} %train_ref.1) | copy-start | bytes 28
  27.7 0.7 %copy-start.2 = (s32[2]{0:T(128)S(1)}, s32[2]{0:T(128)}, u32[]{:S(2)}) copy-start(s32[2]{0:T(128)} %scale_ref.1) | copy-start | bytes 28

commit v8 on v6

--- a/solution.py
+++ b/solution.py
@@ -17,12 +17,12 @@
 
 
 EARLY = 6
-FIRST = 12
+ORDER = (12, *range(12), 13, 14, 15)
 
 
 def sent_to_all(array, axes):
     beams, pulses = (lax.axis_size(axis) for axis in axes)
-    order = [((FIRST + i) % beams) * pulses + j for i in range(beams) for j in range(pulses)]
+    order = [i * pulses + j for i in ORDER for j in range(pulses)]
     copies = jnp.broadcast_to(array, (beams * pulses, *array.shape))
     return lax.all_to_all(
         copies, axes, split_axis=0, concat_axis=0, tiled=True, axis_index_groups=[order]
@@ -148,7 +148,7 @@
         rolled = []
         for part in range(2):
             if chunk < CHUNKS - 1:
-                at = (chunk - FIRST) % (CHUNKS - 1)
+                at = ORDER.index(chunk)
                 line = jnp.broadcast_to(rows[part][at : at + 1, :], (8, TILE))
                 rolled.append(
                     [pltpu.roll(line, 8 * q, 1, stride=1, stride_axis=0) for q in range(16)]

time: 39.3 us -> 39.2 us (level)
  no operation moved by 1% of the time
where the time goes in v8:
time: 39.2 us; the launch traced here: 38.9 us
  starting transfers between devices  25.5 us (65%)
  waiting for transfers between devices  5.93 us (15%)
  Pallas kernels  2.49 us (6%)
  local copies, waits for them, and re-layouts  2.08 us (5%)
  blocking collectives  1.97 us (5%)
  between operations  0.83 us (2%)
    all_to_all x1, starting transfers between devices, sent_to_all(): lax.all_to_all(copies, axes, split_axis=0, concat_axis=0, tiled=True, axi...  13.3 us
    ppermute x4, starting transfers between devices, sent(): return lax.ppermute(array, ('beam', 'range'), inside)  12.2 us
    all_to_all x1, waiting for transfers between devices, sent_to_all(): lax.all_to_all(copies, axes, split_axis=0, concat_axis=0, tiled=True, axi...  5.92 us
    all_gather x1, blocking collectives, strip_of_chip(): return lax.all_gather(mine, 'range', axis_index_groups=chips, tiled=True)  1.97 us
    pallas_call x1, Pallas kernels, body(): pl.pallas_call(detect, out_shape=(jax.ShapeDtypeStruct((2, 8, 2, INNER *...  1.69 us
    unnamed x13, local copies, waits for them, and re-layouts  1.45 us
  transfers between devices with their start and end apart: 5, of which 1 were waited for; matrix products, arithmetic and copies ran while one was open for 2% of the time, Pallas kernels for 2%

profile of v8, /device:TPU:24, one launch (start us, length us, event | category | flops | bytes accessed | tf_op | source)
XLA Modules:
  0.0 38.9 jit_solution(11704329320124279392)
XLA Ops:
  0.6 0.8 %copy.11 = bf16[2,8,2,512]{3,1,2,0:T(8,128)(2,1)S(1)} copy(bf16[2,8,2,512]{3,2,1,0:T(2,128)(2,1)} %param.6) | data formatting | bytes 65536 | tf_op args[0]
  1.4 0.0 copy-start.4
  1.4 2.6 %collective-permute-start = (bf16[2,2,2,8,256]{4,3,2,1,0:T(8,128)(2,1)S(1)}, bf16[2,2,2,8,256]{4,3,2,1,0:T(8,128)(2,1)S(1)}, u32[]{:S(2)}, u32[]{:S(2)}) collective-permute-start(bf16[2,2,2,8,256]{4,3,2,1,0:T(8,128)(2,1)S(1)} %get-tuple-element.17), channel_id=1, source_target_pairs={{2,0},{3,1},{4,2},{5,3},{6,4},{7,5},{34,32},{35,33},{36,34},{37,35... | collective-permute-start | bytes 98312 | tf_op jit(solution)/shard_map/ppermute | solution.py:49
  4.1 0.7 %collective-permute-start.1 = (bf16[2,2,2,8,256]{4,3,2,1,0:T(8,128)(2,1)S(1)}, bf16[2,2,2,8,256]{4,3,2,1,0:T(8,128)(2,1)S(1)}, u32[]{:S(2)}, u32[]{:S(2)}) collective-permute-start(bf16[2,2,2,8,256]{4,3,2,1,0:T(8,128)(2,1)S(1)} %get-tuple-element.17), channel_id=1, source_target_pairs={{194,192},{195,193},{196,194},{197,195},{198,196},{199,197},{226,2... | collective-permute-start | bytes 98312 | tf_op jit(solution)/shard_map/ppermute | solution.py:49
  4.8 6.1 %collective-permute-start.3 = (bf16[1,2,2,8,256]{4,3,2,1,0:T(8,128)(2,1)S(1)}, bf16[1,2,2,8,256]{4,3,2,1,0:T(8,128)(2,1)S(1)}, u32[]{:S(2)}, u32[]{:S(2)}) collective-permute-start(bf16[1,2,2,8,256]{4,3,2,1,0:T(8,128)(2,1)S(1)} %get-tuple-element.18), channel_id=1, source_target_pairs={{6,0},{1,3},{3,5},{5,7},{38,32},{33,35},{35,37},{37,39},{70,64},{6... | collective-permute-start | bytes 49160 | tf_op jit(solution)/shard_map/ppermute | solution.py:49
  10.9 2.7 %collective-permute-start.2 = (bf16[2,2,2,8,256]{4,3,2,1,0:T(8,128)(2,1)S(1)}, bf16[2,2,2,8,256]{4,3,2,1,0:T(8,128)(2,1)S(1)}, u32[]{:S(2)}, u32[]{:S(2)}) collective-permute-start(bf16[2,2,2,8,256]{4,3,2,1,0:T(8,128)(2,1)S(1)} %get-tuple-element.16), channel_id=1, source_target_pairs={{4,0},{5,1},{6,2},{7,3},{36,32},{37,33},{38,34},{39,35},{68,64},{6... | collective-permute-start | bytes 98312 | tf_op jit(solution)/shard_map/ppermute | solution.py:49
  13.7 0.6 %broadcast_in_dim.3 = bf16[64,2,32]{2,1,0:T(2,128)(2,1)} broadcast(bf16[2,32]{1,0:T(2,128)(2,1)S(1)} %copy-done.4), dimensions={1,2} | broadcast | bytes 8320 | tf_op jit(solution)/shard_map/broadcast_in_dim | solution.py:26
  14.3 13.3 %all-to-all-start = ((bf16[64,2,32]{2,1,0:T(2,128)(2,1)}), bf16[64,2,32]{2,1,0:T(2,128)(2,1)S(1)}, u32[]{:S(2)}, u32[]{:S(2)}) async-start(bf16[64,2,32]{2,1,0:T(2,128)(2,1)} %broadcast_in_dim.3), calls=%async_computation | async-start | bytes 65536 | tf_op jit(solution)/shard_map/all_to_all | solution.py:27
  27.7 0.0 copy-start.3
  27.7 0.0 copy-start
  27.7 0.0 copy-start.1
  27.7 0.0 copy-start.2
  27.7 0.6 %copy-done.3 = s32[2]{0:T(128)S(1)} copy-done((s32[2]{0:T(128)S(1)}, s32[2]{0:T(128)}, u32[]{:S(2)}) %copy-start.3) | copy-done | bytes 32
  28.3 0.0 copy-done
  28.3 0.0 copy-done.1
  28.4 0.0 copy-done.2
  28.4 0.7 %tables.1 = (bf16[384,256]{1,0:T(8,128)(2,1)S(1)}, f32[16,512]{1,0:T(8,128)S(1)}, f32[16,128]{1,0:T(8,128)S(1)}, f32[16,128]{1,0:T(8,128)S(1)}, s32[3]{0:T(128)S(4)}) custom-call(s32[1]{0:T(128)} %bitcast.1.place_ref, s32[2]{0:T(128)S(1)} %copy-done, s32[2]{0:T(128)S(1)} %copy-done.1, s32[2]{0:T(128)S(1)} %copy-done.2, s32[2]{0:T(128)S(1)} %copy-done.3), custom_call_target="tpu_custom_call" | custom-call | flops 1048576 | bytes 262144 | tf_op jit(solution)/shard_map/tables/pallas_call | solution.py:232
  29.1 0.0 collective-permute-done
  29.1 0.0 collective-permute-done.2
  29.1 0.0 collective-permute-done.3
  29.2 2.0 %all_gather.3.strip_ref = bf16[14,2,2,8,256]{4,3,2,1,0:T(8,128)(2,1)S(1)} all-gather(bf16[7,2,2,8,256]{4,3,2,1,0:T(8,128)(2,1)S(1)} %fusion), channel_id=1, replica_groups={{0,1},{2,3},{4,5},{6,7},{8,9},{10,11},{12,13},{14,15},{16,17},{18,19},{..., dimensions={0}, use_global_device_ids=true | all-gather | bytes 344064 | tf_op jit(solution)/shard_map/all_gather | solution.py:61
  31.1 0.1 prepare.1
  31.3 5.9 %all-to-all-done = bf16[64,2,32]{2,1,0:T(2,128)(2,1)S(1)} async-done(((bf16[64,2,32]{2,1,0:T(2,128)(2,1)}), bf16[64,2,32]{2,1,0:T(2,128)(2,1)S(1)}, u32[]{:S(2)}, u32[]{:S(2)}) %all-to-all-start) | async-done | bytes 8224 | tf_op jit(solution)/shard_map/all_to_all | solution.py:27
  37.2 1.7 %detect.1 = (bf16[2,8,2,512]{3,2,1,0:T(2,128)(2,1)}, f32[2,8,512]{2,1,0:T(8,128)}) custom-call(bf16[128,32]{1,0:T(8,128)(2,1)S(1)} %bitcast.15, bf16[16,5632]{1,0:T(8,128)(2,1)S(1)} %get-tuple-element.10.left_ref, bf16[16,5632]{1,0:T(8,128)(2,1)S(1)} %get-tuple-element.11.right_ref, bf16[384,256]{1,0:T(8,128)(2,1)S(1)} %get-tuple-element.12.window_ref, ...), custom_call_target="tpu_custom_call" | custom-call | flops 268435456 | bytes 1048576 | tf_op jit(solution)/shard_map/detect/pallas_call | solution.py:257
  (9 shorter events, 0.1 us)
Async XLA Ops:
  1.4 12.2 %copy-start.4 = (bf16[2,32]{1,0:T(2,128)(2,1)S(1)}, bf16[2,32]{1,0:T(2,128)(2,1)}, u32[]{:S(2)}) copy-start(bf16[2,32]{1,0:T(2,128)(2,1)} %param.7) | copy-start | bytes 388
  1.4 27.6 %collective-permute-start = (bf16[2,2,2,8,256]{4,3,2,1,0:T(8,128)(2,1)S(1)}, bf16[2,2,2,8,256]{4,3,2,1,0:T(8,128)(2,1)S(1)}, u32[]{:S(2)}, u32[]{:S(2)}) collective-permute-start(bf16[2,2,2,8,256]{4,3,2,1,0:T(8,128)(2,1)S(1)} %get-tuple-element.17), channel_id=1, source_target_pairs={{2,0},{3,1},{4,2},{5,3},{6,4},{7,5},{34,32},{35,33},{36,34},{37,35... | collective-permute-start | bytes 98312 | tf_op jit(solution)/shard_map/ppermute | solution.py:49
  4.1 25.0 %collective-permute-start.1 = (bf16[2,2,2,8,256]{4,3,2,1,0:T(8,128)(2,1)S(1)}, bf16[2,2,2,8,256]{4,3,2,1,0:T(8,128)(2,1)S(1)}, u32[]{:S(2)}, u32[]{:S(2)}) collective-permute-start(bf16[2,2,2,8,256]{4,3,2,1,0:T(8,128)(2,1)S(1)} %get-tuple-element.17), channel_id=1, source_target_pairs={{194,192},{195,193},{196,194},{197,195},{198,196},{199,197},{226,2... | collective-permute-start | bytes 98312 | tf_op jit(solution)/shard_map/ppermute | solution.py:49
  4.8 24.4 %collective-permute-start.3 = (bf16[1,2,2,8,256]{4,3,2,1,0:T(8,128)(2,1)S(1)}, bf16[1,2,2,8,256]{4,3,2,1,0:T(8,128)(2,1)S(1)}, u32[]{:S(2)}, u32[]{:S(2)}) collective-permute-start(bf16[1,2,2,8,256]{4,3,2,1,0:T(8,128)(2,1)S(1)} %get-tuple-element.18), channel_id=1, source_target_pairs={{6,0},{1,3},{3,5},{5,7},{38,32},{33,35},{35,37},{37,39},{70,64},{6... | collective-permute-start | bytes 49160 | tf_op jit(solution)/shard_map/ppermute | solution.py:49
  10.9 18.2 %collective-permute-start.2 = (bf16[2,2,2,8,256]{4,3,2,1,0:T(8,128)(2,1)S(1)}, bf16[2,2,2,8,256]{4,3,2,1,0:T(8,128)(2,1)S(1)}, u32[]{:S(2)}, u32[]{:S(2)}) collective-permute-start(bf16[2,2,2,8,256]{4,3,2,1,0:T(8,128)(2,1)S(1)} %get-tuple-element.16), channel_id=1, source_target_pairs={{4,0},{5,1},{6,2},{7,3},{36,32},{37,33},{38,34},{39,35},{68,64},{6... | collective-permute-start | bytes 98312 | tf_op jit(solution)/shard_map/ppermute | solution.py:49
  14.3 22.9 %all-to-all-start = ((bf16[64,2,32]{2,1,0:T(2,128)(2,1)}), bf16[64,2,32]{2,1,0:T(2,128)(2,1)S(1)}, u32[]{:S(2)}, u32[]{:S(2)}) async-start(bf16[64,2,32]{2,1,0:T(2,128)(2,1)} %broadcast_in_dim.3), calls=%async_computation | async-start | bytes 65536 | tf_op jit(solution)/shard_map/all_to_all | solution.py:27
  27.7 0.7 %copy-start.3 = (s32[2]{0:T(128)S(1)}, s32[2]{0:T(128)}, u32[]{:S(2)}) copy-start(s32[2]{0:T(128)} %offset_ref.1) | copy-start | bytes 28
  27.7 0.7 %copy-start = (s32[2]{0:T(128)S(1)}, s32[2]{0:T(128)}, u32[]{:S(2)}) copy-start(s32[2]{0:T(128)} %guard_ref.1) | copy-start | bytes 28
  27.7 0.7 %copy-start.1 = (s32[2]{0:T(128)S(1)}, s32[2]{0:T(128)}, u32[]{:S(2)}) copy-start(s32[2]{0:T(128)} %train_ref.1) | copy-start | bytes 28
  27.7 0.7 %copy-start.2 = (s32[2]{0:T(128)S(1)}, s32[2]{0:T(128)}, u32[]{:S(2)}) copy-start(s32[2]{0:T(128)} %scale_ref.1) | copy-start | bytes 28
